TPU v7x, 256 devices: a whole 4x4x8 slice. The times are simulated.
256 devices in a mesh: dp: 4 (over x), seq: 8 (over y, core), tp: 8 (over z).
Axes of the slice: x: 4, y: 4, z: 8, core: 2. Of those that a mesh axis runs over, the one named last changes fastest.
Arguments:
- queries: bfloat16 [16384, 4096], P(('dp', 'seq'), 'tp'), parts along dimension 0, may hold values from -181 to 181
- rotated_key_states: bfloat16 [16384, 1024], P(('dp', 'seq'), 'tp'), parts along dimension 0, may hold values from -6.1 to 6.1
- value_state_vectors: bfloat16 [16384, 1024], P(('dp', 'seq'), 'tp'), parts along dimension 0, may hold values from -6 to 6
- out_weight: bfloat16 [4096, 8192], P('tp'), may hold values from -0.15625 to 0.15625
- residual: bfloat16 [16384, 8192], P(('dp', 'seq', 'tp')), parts along dimension 0, may hold values from -0.75 to 0.75
- norm_gain: bfloat16 [8192], replicated, may hold values from 0.099609375 to 2
Outputs:
- new_residual: bfloat16 [16384, 8192], P(('dp', 'seq', 'tp')), parts along dimension 0
- next_input: bfloat16 [16384, 8192], P(('dp', 'seq', 'tp')), parts along dimension 0
There are 4 independent parts, one for each index of `dp`. A program takes and returns all parts, laid end to end along the dimension named above; an argument that names none is the same for every part. Nothing has to cross between parts.
All inputs are finite; a program needn't handle non-finite values.
Results may differ from a plain program's by a relative error of at most 0.025.
Values may be sent and summed in bfloat16 or wider, within the bound.
A program may use at most 192 MiB of HBM per device.

v0:
```python
import jax
import jax.numpy as jnp
from jax import lax
from jax.sharding import PartitionSpec as P

D = 8192
HEAD_SIZE = 128


softness = 0.9
scale_floor = 256.0
neg_large = -1e30


def copy_for_each(value, axis):
    devices = lax.axis_size(axis)
    return lax.all_to_all(
        jnp.broadcast_to(value[None], (devices, *value.shape)), axis, 0, 0, tiled=True
    )


def joined_along(blocks, dim):
    dims = list(blocks.shape[1:])
    dims[dim] *= blocks.shape[0]
    return jnp.moveaxis(blocks, 0, dim).reshape(dims)


def gather_directly(value, axis, dim):
    blocks = copy_for_each(value, axis)
    return joined_along(blocks, dim)


def of_everyone(value, axis):
    everything = copy_for_each(value, axis)
    return jnp.max(everything, axis=0)


def in_one(arrays, axis):
    ends = [0]
    for a in arrays:
        ends.append(ends[-1] + a.size)
    total = of_everyone(jnp.concatenate([a.ravel() for a in arrays]), axis)
    return tuple((total[b:e].reshape(a.shape) for a, b, e in zip(arrays, ends, ends[1:])))


def soft_grid(values):
    return values - softness * jnp.sin(jnp.pi * values) / jnp.pi


def fake_quant(blocks, block_axis, peak):
    block_max = jnp.max(jnp.abs(blocks), axis=block_axis, keepdims=True)
    tensor_scale = peak / (6.0 * 448.0)
    block_scale = jnp.maximum(block_max / (6.0 * tensor_scale), scale_floor).astype(jnp.bfloat16)
    block_scale = lax.optimization_barrier(block_scale).astype(jnp.float32)
    spacing = block_scale * tensor_scale
    payload = soft_grid(blocks / spacing).astype(jnp.bfloat16)
    payload = lax.optimization_barrier(payload).astype(jnp.float32)
    return (payload * spacing).astype(jnp.bfloat16)


def attend_piece(attn_state, q_grouped, kv_piece, query_pos, causal_piece):
    running_max, running_total, running_sum = attn_state
    kv_heads = q_grouped.shape[1]
    piece_rows = kv_piece.shape[1]
    keys_split = kv_piece[0].reshape(piece_rows, kv_heads, HEAD_SIZE)
    values_split = kv_piece[1].reshape(piece_rows, kv_heads, HEAD_SIZE)
    scores = jnp.einsum(
        "tkgd,skd->kgts", q_grouped, keys_split, preferred_element_type=jnp.float32
    ) * HEAD_SIZE ** (-0.5)
    if causal_piece:
        key_pos = lax.broadcasted_iota(jnp.int32, (1, piece_rows), 1)
        allowed = query_pos[:, None] >= key_pos
        masked = jnp.where(allowed, scores, neg_large)
        new_max = jnp.maximum(running_max, jnp.max(masked, axis=3))
        weights = jnp.where(allowed, jnp.exp(masked - new_max[..., None]), 0.0)
    else:
        new_max = jnp.maximum(running_max, jnp.max(scores, axis=3))
        weights = jnp.exp(scores - new_max[..., None])
    shrink_factor = jnp.exp(running_max - new_max)
    running_total = running_total * shrink_factor + jnp.sum(weights, axis=3)
    running_sum = running_sum * shrink_factor[..., None] + jnp.einsum(
        "kgts,skd->kgtd",
        weights.astype(jnp.bfloat16),
        values_split,
        preferred_element_type=jnp.float32,
    )
    return (new_max, running_total, running_sum)


def local(queries, rotated_key_states, value_state_vectors, out_weight, residual, norm_gain):
    token_count = queries.shape[0]
    kv_heads = rotated_key_states.shape[1] // HEAD_SIZE
    grouped_heads = queries.shape[1] // HEAD_SIZE // kv_heads
    seq_rank = lax.axis_index("seq")
    q_grouped = queries.reshape(token_count, kv_heads, grouped_heads, HEAD_SIZE)
    first_query = seq_rank * token_count
    last_query = first_query + token_count - 1
    query_pos = first_query + lax.broadcasted_iota(jnp.int32, (token_count,), 0)
    kv_own = jnp.stack((rotated_key_states, value_state_vectors))
    start_state = (
        jnp.full((kv_heads, grouped_heads, token_count), neg_large, jnp.float32),
        jnp.zeros((kv_heads, grouped_heads, token_count), jnp.float32),
        jnp.zeros((kv_heads, grouped_heads, token_count, HEAD_SIZE), jnp.float32),
    )

    def fold_piece(attn_state, kv_piece, first_row):
        piece_rows = kv_piece.shape[1]

        def before_queries(state_in):
            return attend_piece(state_in, q_grouped, kv_piece, query_pos, False)

        def across_queries(state_in):
            return attend_piece(state_in, q_grouped, kv_piece, query_pos, True)

        def after_queries(state_in):
            return state_in

        branch_index = jnp.where(
            first_row + piece_rows <= first_query, 0, jnp.where(first_row <= last_query, 1, 2)
        ).astype(jnp.int32)
        return lax.switch(branch_index, [before_queries, across_queries, after_queries], attn_state)

    final_state = fold_piece(start_state, gather_directly(kv_own, "seq", 1), jnp.int32(0))
    attended = (final_state[2] / final_state[1][..., None]).astype(jnp.bfloat16)
    features = attended.shape[0] * attended.shape[1] * HEAD_SIZE
    act_t = attended.transpose(0, 1, 3, 2).reshape(features, token_count).astype(jnp.float32)
    weight_f = out_weight.astype(jnp.float32)
    act_local = jnp.max(jnp.abs(act_t))
    weight_local = jnp.max(jnp.abs(weight_f))
    act_peak, weight_peak = in_one((act_local, weight_local), ("seq", "tp"))
    act_q = fake_quant(act_t.reshape(features // 16, 16, token_count), 1, act_peak).reshape(
        features, token_count
    )
    weight_q = fake_quant(weight_f.reshape(features // 16, 16, D), 1, weight_peak).reshape(
        features, D
    )
    share_rows = token_count // lax.axis_size("tp")
    projected = lax.psum_scatter(
        lax.dot_general(
            act_q, weight_q, (((0,), (0,)), ((), ())), preferred_element_type=jnp.float32
        ).astype(jnp.bfloat16),
        "tp",
        scatter_dimension=0,
        tiled=True,
    ).astype(jnp.float32)
    hidden_sum = residual.astype(jnp.float32) + projected
    new_residual = hidden_sum.astype(jnp.bfloat16)
    mean_square = jnp.mean(hidden_sum * hidden_sum, axis=1, keepdims=True)
    normed = hidden_sum * lax.rsqrt(mean_square + 1e-05) * norm_gain.astype(jnp.float32)
    norm_peak = of_everyone(jnp.max(jnp.abs(normed)), ("seq", "tp"))
    next_input = fake_quant(normed.reshape(share_rows, D // 16, 16), 2, norm_peak).reshape(
        share_rows, D
    )
    return (new_residual, next_input)


def solution(mesh):
    in_specs = (
        P(("dp", "seq"), "tp"),
        P(("dp", "seq"), "tp"),
        P(("dp", "seq"), "tp"),
        P("tp", None),
        P(("dp", "seq", "tp"), None),
        P(),
    )
    out_specs = (P(("dp", "seq", "tp"), None), P(("dp", "seq", "tp"), None))
    return jax.shard_map(local, mesh=mesh, in_specs=in_specs, out_specs=out_specs, check_vma=False)
```

profile of v0, /device:TPU:1, one launch (start us, length us, event | category | flops | bytes accessed | tf_op | source)
XLA Modules:
  0.0 337.8 jit_solution(7261904593748596)
XLA Ops:
  7.2 1.0 pad_maximum_fusion
  8.2 1.8 broadcast_in_dim.43
  9.9 6.7 %all-to-all-start = ((bf16[8,2,512,128]{3,2,1,0:T(8,128)(2,1)}), bf16[8,2,512,128]{3,2,1,0:T(8,128)(2,1)S(1)}, u32[]{:S(2)}, u32[]{:S(2)}) async-start(bf16[8,2,512,128]{3,2,1,0:T(8,128)(2,1)} %broadcast_in_dim.43), calls=%async_computation | async-start | bytes 4194304 | tf_op jit(solution)/shard_map/all_to_all | solution.py:17
  16.6 1.3 copy.50
  17.9 5.2 %abs_reduce_fusion.1 = f32[]{:T(128)} fusion(bf16[512,8192]{1,0:T(8,128)(2,1)} %param.12), kind=kLoop, calls=%fused_computation.47 | loop fusion | flops 12582911 | bytes 8388612 | tf_op jit(solution)/shard_map/reduce_max | solution.py:129
  23.1 13.4 %abs_reduce_fusion = (f32[32,8192]{1,0:T(8,128)}, f32[512,8192]{1,0:T(8,128)}) fusion(bf16[512,8192]{1,0:T(8,128)(2,1)} %param.12), kind=kLoop, calls=%fused_computation.46 | loop fusion | flops 12320768 | bytes 26214400 | tf_op jit(solution)/shard_map/reduce_max | solution.py:51
  36.5 6.4 %all-to-all-done = bf16[8,2,512,128]{3,2,1,0:T(8,128)(2,1)S(1)} async-done(((bf16[8,2,512,128]{3,2,1,0:T(8,128)(2,1)}), bf16[8,2,512,128]{3,2,1,0:T(8,128)(2,1)S(1)}, u32[]{:S(2)}, u32[]{:S(2)}) %all-to-all-start) | async-done | bytes 2097184 | tf_op jit(solution)/shard_map/all_to_all | solution.py:17
  43.0 49.1 %conditional.1 = (f32[1,4,512]{2,1,0:T(4,128)S(1)}, f32[1,4,512,128]{2,3,1,0:T(8,128)S(1)}) conditional(s32[]{:T(128)} %clamp.3, (bf16[2,4096,128]{2,1,0:T(8,128)(2,1)S(1)}, bf16[512,1,4,128]{0,3,2,1:T(8,128)(2,1)S(1)}) %tuple.58, (s32[]{:T(128)}, s32[512]{0:T(512)S(1)}, bf16[2,4096,128]{2,1,0:T(8,128)(2,1)S(1)}, ...), branch_computations={%region_0.3_spmd, %region_3.6_spmd, %region_6.7_spmd} | conditional | flops 4406385152 | bytes 131692616 | solution.py:121
  43.1 1.7 iota_compare_fusion
  44.8 13.9 %fusion.19 = (f32[4,512]{1,0:T(4,128)S(1)}, f32[4096,512,4]{1,0,2:T(8,128)}) fusion(pred[512,4096]{0,1:T(8,128)(4,1)S(1)} %iota_compare_fusion, bf16[512,1,4,128]{0,3,2,1:T(8,128)(2,1)S(1)} %get-tuple-element.63, bf16[2,4096,128]{2,1,0:T(8,128)(2,1)S(1)} %get-tuple-element.18), kind=kOutput, calls=%fused_computation.21 | convolution fusion | flops 2172647424 | bytes 37232640 | tf_op jit(solution)/shard_map/cond/branch_1_fun/tkgd,skd->kgts/dot_general | solution.py:67
  58.7 15.2 %fusion.21 = f32[4,512]{1,0:T(4,128)S(1)} fusion(f32[4096,512,4]{1,0,2:T(8,128)} %get-tuple-element.80, f32[4,512]{1,0:T(4,128)S(1)} %broadcast_maximum_fusion.1, pred[512,4096]{0,1:T(8,128)(4,1)S(1)} %iota_compare_fusion), kind=kLoop, calls=%fused_computation.23 | loop fusion | flops 41940992 | bytes 35667968 | tf_op jit(solution)/shard_map/cond/branch_1_fun/reduce_sum | solution.py:80
  73.9 16.7 %fusion.29 = f32[1,4,512,128]{3,2,1,0:T(8,128)} fusion(f32[4096,512,4]{1,0,2:T(8,128)} %get-tuple-element.80, f32[4,512]{1,0:T(4,128)S(1)} %broadcast_maximum_fusion.1, pred[512,4096]{0,1:T(8,128)(4,1)S(1)} %iota_compare_fusion, bf16[2,4096,128]{2,1,0:T(8,128)(2,1)S(1)} %copy-done.1, f32[4,512]{1,0:T(4,128)S(1)} %get-tuple-element.77), kind=kOutput, calls=%fused_computation.29 | convolution fusion | flops 2189688832 | bytes 37765120 | tf_op jit(solution)/shard_map/cond/branch_1_fun/kgts,skd->kgtd/dot_general | solution.py:81
  90.6 1.6 copy.61
  92.2 1.0 copy-done.2
  93.1 2.0 abs_reduce_fusion.4
  95.1 1.4 pad_maximum_fusion.1
  97.1 9.8 %all-to-all-start.1 = ((f32[64,1,2]{2,1,0:T(1,128)}), f32[64,1,2]{2,1,0:T(1,128)S(1)}, u32[]{:S(2)}, u32[]{:S(2)}) async-start(f32[64,1,2]{2,1,0:T(1,128)} %broadcast_in_dim.44), calls=%async_computation.1 | async-start | bytes 65536 | tf_op jit(solution)/shard_map/all_to_all | solution.py:17
  107.2 8.9 %all-to-all-done.1 = f32[64,1,2]{2,1,0:T(1,128)S(1)} async-done(((f32[64,1,2]{2,1,0:T(1,128)}), f32[64,1,2]{2,1,0:T(1,128)S(1)}, u32[]{:S(2)}, u32[]{:S(2)}) %all-to-all-start.1) | async-done | bytes 544 | tf_op jit(solution)/shard_map/all_to_all | solution.py:17
  119.6 3.9 %subtract_convert_fusion.2 = bf16[32,16,512]{2,1,0:T(8,128)(2,1)S(1)} fusion(f32[32,16,512]{2,1,0:T(8,128)S(1)} %bitcast.129, f32[32,512]{1,0:T(8,128)S(1)} %multiply_bitcast_fusion.2), kind=kLoop, calls=%fused_computation.60 | loop fusion | flops 1310720 | bytes 1638400 | tf_op jit(solution)/shard_map/convert_element_type | solution.py:56
  123.5 1.3 fusion.45
  124.9 60.0 %subtract_convert_fusion = bf16[32,16,8192]{2,1,0:T(8,128)(2,1)} fusion(f32[32,8192]{1,0:T(8,128)S(1)} %multiply_bitcast_fusion, f32[512,8192]{1,0:T(8,128)} %get-tuple-element.72), kind=kLoop, calls=%fused_computation.45 | loop fusion | flops 20971520 | bytes 26214400 | tf_op jit(solution)/shard_map/convert_element_type | solution.py:56
  185.0 10.6 %bitcast_convert_fusion = bf16[512,8192]{1,0:T(8,128)(2,1)} fusion(bf16[32,16,8192]{2,1,0:T(8,128)(2,1)} %subtract_convert_fusion, f32[32,8192]{1,0:T(8,128)S(1)} %multiply_bitcast_fusion, bf16[32,16,512]{2,1,0:T(8,128)(2,1)S(1)} %subtract_convert_fusion.2, f32[32,512]{1,0:T(8,128)S(1)} %multiply_bitcast_fusion.2), kind=kOutput, calls=%fused_computation.43 | convolution fusion | flops 4312530944 | bytes 18415616 | tf_op jit(solution)/shard_map/dot_general | solution.py:139
  195.6 89.7 %reduce-scatter.2.cloned.1.call-done = bf16[64,8192]{1,0:T(8,128)(2,1)} async-done(((bf16[512,8192]{1,0:T(8,128)(2,1)}), bf16[64,8192]{1,0:T(8,128)(2,1)}) %reduce-scatter.2.cloned.1.call-update) | async-done | bytes 1048592 | tf_op jit(solution)/shard_map/reduce_scatter | solution.py:138
  285.3 1.7 multiply_reduce_fusion
  287.0 3.2 abs_reduce_fusion.3
  290.2 2.7 copy.55
  292.9 1.2 broadcast_in_dim.45
  294.1 8.1 %all-to-all-start.2 = ((f32[64,1,1]{2,1,0:T(1,128)}), f32[64,1,1]{2,1,0:T(1,128)S(1)}, u32[]{:S(2)}, u32[]{:S(2)}) async-start(f32[64,1,1]{2,1,0:T(1,128)} %broadcast_in_dim.45), calls=%async_computation.3 | async-start | bytes 65536 | tf_op jit(solution)/shard_map/all_to_all | solution.py:17
  302.2 3.2 abs_reduce_fusion.2
  305.5 5.9 %all-to-all-done.2 = f32[64,1,1]{2,1,0:T(1,128)S(1)} async-done(((f32[64,1,1]{2,1,0:T(1,128)}), f32[64,1,1]{2,1,0:T(1,128)S(1)}, u32[]{:S(2)}, u32[]{:S(2)}) %all-to-all-start.2) | async-done | bytes 288 | tf_op jit(solution)/shard_map/all_to_all | solution.py:17
  313.4 15.4 %subtract_convert_fusion.1 = bf16[64,512,16]{0,2,1:T(8,128)(2,1)S(1)} fusion(f32[64,512]{0,1:T(8,128)S(1)} %multiply_bitcast_fusion.1, f32[64,8192]{0,1:T(8,128)} %copy.55), kind=kLoop, calls=%fused_computation.50 | loop fusion | flops 2621440 | bytes 3276800 | tf_op jit(solution)/shard_map/convert_element_type | solution.py:56
  329.3 1.6 copy.57
  (29 shorter events, 3.1 us)
Async XLA Ops:
  9.9 32.9 %all-to-all-start = ((bf16[8,2,512,128]{3,2,1,0:T(8,128)(2,1)}), bf16[8,2,512,128]{3,2,1,0:T(8,128)(2,1)S(1)}, u32[]{:S(2)}, u32[]{:S(2)}) async-start(bf16[8,2,512,128]{3,2,1,0:T(8,128)(2,1)} %broadcast_in_dim.43), calls=%async_computation | async-start | bytes 4194304 | tf_op jit(solution)/shard_map/all_to_all | solution.py:17
  43.0 15.7 %copy-start = (bf16[2,4096,128]{2,1,0:T(8,128)(2,1)}, bf16[2,4096,128]{2,1,0:T(8,128)(2,1)S(1)}, u32[]{:S(2)}) copy-start(bf16[2,4096,128]{2,1,0:T(8,128)(2,1)S(1)} %get-tuple-element.18) | copy-start | bytes 6291460 | tf_op jit(solution)/shard_map/cond
  58.7 15.2 %copy-start.1 = (bf16[2,4096,128]{2,1,0:T(8,128)(2,1)S(1)}, bf16[2,4096,128]{2,1,0:T(8,128)(2,1)}, u32[]{:S(2)}) copy-start(bf16[2,4096,128]{2,1,0:T(8,128)(2,1)} %copy-done) | copy-start | bytes 6291460 | tf_op jit(solution)/shard_map/cond
  92.2 1.0 copy-start.2
  97.1 19.0 %all-to-all-start.1 = ((f32[64,1,2]{2,1,0:T(1,128)}), f32[64,1,2]{2,1,0:T(1,128)S(1)}, u32[]{:S(2)}, u32[]{:S(2)}) async-start(f32[64,1,2]{2,1,0:T(1,128)} %broadcast_in_dim.44), calls=%async_computation.1 | async-start | bytes 65536 | tf_op jit(solution)/shard_map/all_to_all | solution.py:17
  107.0 178.3 %reduce-scatter.2.cloned.1.call-start = ((), (), s32[]{:S(2)}) async-start(), calls=%async_computation.4 | async-start | bytes 9437184 | tf_op jit(solution)/shard_map/reduce_scatter | solution.py:138
  184.9 10.6 %copy-start.4 = (bf16[8192]{0:T(1024)(128)(2,1)S(1)}, bf16[8192]{0:T(1024)(128)(2,1)}, u32[]{:S(2)}) copy-start(bf16[8192]{0:T(1024)(128)(2,1)} %param.14) | copy-start | bytes 49156
  184.9 100.3 %copy-start.3 = (bf16[64,8192]{1,0:T(8,128)(2,1)S(1)}, bf16[64,8192]{1,0:T(8,128)(2,1)}, u32[]{:S(2)}) copy-start(bf16[64,8192]{1,0:T(8,128)(2,1)} %param.13) | copy-start | bytes 3145732
  294.1 17.3 %all-to-all-start.2 = ((f32[64,1,1]{2,1,0:T(1,128)}), f32[64,1,1]{2,1,0:T(1,128)S(1)}, u32[]{:S(2)}, u32[]{:S(2)}) async-start(f32[64,1,1]{2,1,0:T(1,128)} %broadcast_in_dim.45), calls=%async_computation.3 | async-start | bytes 65536 | tf_op jit(solution)/shard_map/all_to_all | solution.py:17
Sparse Core Ops, SparseCore 0:
  195.7 89.5 reduce-scatter.1
where the time goes:
time: 339 us; the launch traced here: 338 us
  other arithmetic  130 us (38%)
  waiting for transfers between devices  111 us (33%)
  matrix products  41.2 us (12%)
  starting transfers between devices  24.7 us (7%)
  between operations  18.2 us (5%)
  local copies, waits for them, and re-layouts  12.6 us (4%)
    reduce_scatter x1, waiting for transfers between devices, local(): lax.psum_scatter(lax.dot_general(act_q, weight_q, (((0,), (0,)), ((), ())...  89.7 us
    convert_element_type x3, other arithmetic, fake_quant(): payload = soft_grid(blocks / spacing).astype(jnp.bfloat16)  79.4 us
    all_to_all x3, starting transfers between devices, copy_for_each(): lax.all_to_all(jnp.broadcast_to(value[None], (devices, *value.shape)), ax...  24.6 us
    all_to_all x3, waiting for transfers between devices, copy_for_each(): lax.all_to_all(jnp.broadcast_to(value[None], (devices, *value.shape)), ax...  21.3 us
    reduce_max x3, other arithmetic, fake_quant(): block_max = jnp.max(jnp.abs(blocks), axis=block_axis, keepdims=True)  16.8 us
    dot_general x1, matrix products, attend_piece(): jnp.einsum('kgts,skd->kgtd', weights.astype(jnp.bfloat16), values_split,...  16.7 us
    reduce_sum x1, other arithmetic, attend_piece(): running_total = running_total * shrink_factor + jnp.sum(weights, axis=3)  15.2 us
    dot_general x1, matrix products, attend_piece(): jnp.einsum('tkgd,skd->kgts', q_grouped, keys_split, preferred_element_typ...  13.9 us
  transfers between devices with their start and end apart: 4, of which 4 were waited for; matrix products, arithmetic and copies ran while one was open for 7% of the time, Pallas kernels for 0%

commit v1 on v0

v1 whole, which is shorter than its diff:
```python
import jax
import jax.numpy as jnp
from jax import lax
from jax.experimental import pallas as pl
from jax.experimental.pallas import tpu as pltpu
from jax.sharding import PartitionSpec as P

D = 8192
HEAD = 128
SOFT = 0.9
FLOOR = 256.0
NEG = -1e30
MESH = pl.DeviceIdType.MESH
F32 = jnp.float32
BF16 = jnp.bfloat16

TOK = 512
HEADS = 4
FEAT = HEADS * HEAD
NTP = 8
NSEQ = 8
NDP = 4
OWN = TOK // NTP
COLS = D // NSEQ
SUB = COLS // NDP
RA = 368
SCALE = HEAD ** (-0.5) * 1.4426950408889634

QCO = (
    -0.00012284770491532981,
    0.00218366552144289,
    -0.02393284998834133,
    0.16680589318275452,
    -0.6449338793754578,
    1.0,
)


def soft_grid(u):
    w = u - 2.0 * jnp.round(u * 0.5)
    z = w * w
    q = jnp.full_like(z, QCO[0])
    for co in QCO[1:]:
        q = q * z + co
    return u - SOFT * (w * ((1.0 - z) * q))


def quantized(x, block_max, peak):
    tensor_scale = peak / (6.0 * 448.0)
    block_scale = jnp.maximum(block_max / (6.0 * tensor_scale), FLOOR).astype(BF16).astype(F32)
    spacing = block_scale * tensor_scale
    payload = soft_grid(x / spacing).astype(BF16).astype(F32)
    return (payload * spacing).astype(BF16)


def lane_block_max(x):
    for sh in (1, 2, 4, 8):
        x = jnp.maximum(x, pltpu.roll(x, sh, 1))
    lane = lax.broadcasted_iota(jnp.int32, x.shape, 1)
    x = jnp.where(lane % 16 == 15, x, 0.0)
    for sh in (1, 2, 4, 8):
        x = jnp.maximum(x, pltpu.roll(x, 128 - sh, 1))
    return x


class Copies:
    def __init__(self, send_sems, recv_sems):
        self.send_sems, self.recv_sems, self.started = send_sems, recv_sems, []

    def start(self, src, dst, dev, landing):
        i = len(self.started)
        out = pltpu.make_async_remote_copy(
            src_ref=src,
            dst_ref=dst,
            send_sem=self.send_sems.at[i],
            recv_sem=self.recv_sems.at[i],
            device_id=dev,
            device_id_type=MESH,
        )
        out.start()
        back = pltpu.make_async_remote_copy(
            src_ref=landing,
            dst_ref=landing,
            send_sem=self.send_sems.at[i],
            recv_sem=self.recv_sems.at[i],
            device_id=dev,
            device_id_type=MESH,
        )
        self.started.append(out)
        return back

    def finish(self):
        for out in self.started:
            out.wait_send()


N_COPIES = 160


def kernel(
    q_hbm,
    k_hbm,
    v_hbm,
    w_hbm,
    res_hbm,
    gain_ref,
    new_ref,
    next_ref,
    q_buf,
    kv_buf,
    w_stage,
    w_slice,
    w_all,
    vt_buf,
    m_ref,
    l_ref,
    o_ref,
    att_buf,
    z_buf,
    act_all,
    out_buf,
    part_buf,
    res_buf,
    hid_buf,
    tiles,
    send_sems,
    recv_sems,
    local_sems,
):
    dd, ss, tt = lax.axis_index("dp"), lax.axis_index("seq"), lax.axis_index("tp")
    yy = lax.div(ss, 2)
    cc = ss - 2 * yy

    def sid(dy, dc):
        return lax.rem(yy + dy + 4, 4) * 2 + (cc if dc == 0 else 1 - cc)

    def zt(k):
        return lax.rem(tt + k + 2 * NTP, NTP)

    def sq(k):
        return lax.rem(ss + k + 2 * NSEQ, NSEQ)

    def xd(k):
        return lax.rem(dd + k + 2 * NDP, NDP)

    loads = [
        pltpu.make_async_copy(k_hbm, kv_buf.at[ss, 0], local_sems.at[0]),
        pltpu.make_async_copy(v_hbm, kv_buf.at[ss, 1], local_sems.at[1]),
        pltpu.make_async_copy(q_hbm, q_buf, local_sems.at[2]),
        pltpu.make_async_copy(
            w_hbm.at[:, pl.ds(pl.multiple_of(ss * COLS + dd * SUB, SUB), SUB)],
            w_slice,
            local_sems.at[3],
        ),
    ]
    for i in range(4):
        loads.append(
            pltpu.make_async_copy(
                w_hbm.at[pl.ds(i * 128, 128)], w_stage.at[pl.ds(i * 128, 128)], local_sems.at[4 + i]
            )
        )
    loads.append(pltpu.make_async_copy(res_hbm, res_buf, local_sems.at[8]))
    for load in loads:
        load.start()

    barrier = pltpu.get_barrier_semaphore()
    for k in range(1, NTP):
        pl.semaphore_signal(barrier, inc=1, device_id={"tp": zt(k)}, device_id_type=MESH)
    for k in range(1, NSEQ):
        pl.semaphore_signal(barrier, inc=1, device_id={"seq": sq(k)}, device_id_type=MESH)
    for k in (1, 3):
        pl.semaphore_signal(barrier, inc=1, device_id={"dp": xd(k)}, device_id_type=MESH)
    pl.semaphore_wait(barrier, NTP - 1 + NSEQ - 1 + 2)

    copies = Copies(send_sems, recv_sems)

    class SeqGather:
        def __init__(self, unit, half):
            self.unit, self.half = unit, half
            own = unit(sid(0, 0))
            self.x1 = copies.start(own, own, {"seq": sid(1, 0)}, unit(sid(-1, 0)))
            self.x2 = copies.start(own, own, {"seq": sid(-1, 0)}, unit(sid(1, 0)))
            self.x0 = copies.start(own, own, {"seq": sid(0, 1)}, unit(sid(0, 1)))

        def low(self):
            self.x1.wait_recv()
            got, part = self.unit(sid(-1, 0)), self.half(sid(-1, 0), 0)
            self.x4 = copies.start(part, part, {"seq": sid(1, 0)}, self.half(sid(2, 0), 0))
            self.x3 = copies.start(got, got, {"seq": sid(0, 1)}, self.unit(sid(-1, 1)))

        def high(self):
            self.x2.wait_recv()
            got, part = self.unit(sid(1, 0)), self.half(sid(1, 0), 1)
            self.x6 = copies.start(part, part, {"seq": sid(-1, 0)}, self.half(sid(2, 0), 1))
            self.x5 = copies.start(got, got, {"seq": sid(0, 1)}, self.unit(sid(1, 1)))

        def far(self):
            self.x4.wait_recv()
            self.x6.wait_recv()
            got = self.unit(sid(2, 0))
            self.x7 = copies.start(got, got, {"seq": sid(0, 1)}, self.unit(sid(2, 1)))

    def spread_tile(src, dst_of, axis, at):
        me = tt if axis == "tp" else ss
        return [
            copies.start(tiles.at[src], tiles.at[dst_of + me], {axis: at(k)}, tiles.at[dst_of + at(-k)])
            for k in range(1, 8)
        ]

    def max_of_tiles(first):
        top = tiles[first]
        for i in range(1, 8):
            top = jnp.maximum(top, tiles[first + i])
        return top

    loads[0].wait()
    loads[1].wait()
    kv = SeqGather(lambda i: kv_buf.at[i], lambda i, h: kv_buf.at[i, h])

    tiles[48] = jnp.zeros((8, 128), F32)
    for i in range(4):
        loads[4 + i].wait()

        @pl.loop(0, 16)
        def _(j, i=i):
            top = tiles[48]
            piece = jnp.abs(w_stage[i * 128 : (i + 1) * 128, pl.ds(pl.multiple_of(j * 512, 512), 512)].astype(F32))
            top4 = jnp.max(piece.reshape(16, 8, 512), axis=0)
            for n in range(4):
                top = jnp.maximum(top, top4[:, n * 128 : (n + 1) * 128])
            tiles[48] = top

    tiles[8 + tt] = tiles[48]
    w_top = spread_tile(48, 8, "tp", zt)

    def attend(block, kind):
        k_blk = kv_buf[block, 0]
        vt_buf[...] = kv_buf[block, 1].T

        @pl.loop(0, HEADS)
        def _(h):
            q_h = q_buf[:, pl.ds(pl.multiple_of(h * HEAD, HEAD), HEAD)]
            sc = lax.dot_general(k_blk, q_h, (((1,), (1,)), ((), ())), preferred_element_type=F32)
            if kind == "own":
                key = lax.broadcasted_iota(jnp.int32, (TOK, TOK), 0)
                query = lax.broadcasted_iota(jnp.int32, (TOK, TOK), 1)
                sc = jnp.where(key <= query, sc, NEG)
            top = jnp.max(sc, axis=0, keepdims=True)
            if kind != "own":
                old = m_ref[h]
                top = jnp.maximum(old, top)
            p = jnp.exp2((sc - top) * SCALE)
            total = jnp.sum(p, axis=0, keepdims=True)
            o = lax.dot_general(
                vt_buf[...], p.astype(BF16), (((1,), (0,)), ((), ())), preferred_element_type=F32
            )
            if kind != "own":
                shrink = jnp.exp2((old - top) * SCALE)
                total = total + l_ref[h] * shrink
                o = o + o_ref[h] * shrink
            m_ref[h] = top
            l_ref[h] = total
            o_ref[h] = o

    def attend_if_before(block):
        @pl.when(block < ss)
        def _():
            attend(block, "before")

    loads[2].wait()
    attend(ss, "own")

    loads[3].wait()
    for cp in w_top:
        cp.wait_recv()
    w_peak = jnp.max(max_of_tiles(8))

    @pl.loop(0, 8)
    def _(i):
        rows = pl.ds(pl.multiple_of(i * 64, 64), 64)
        x = w_slice[rows, :].astype(F32).reshape(4, 16, SUB)
        top = jnp.max(jnp.abs(x), axis=1, keepdims=True)
        top = jnp.broadcast_to(top, x.shape)
        w_all[dd, pl.ds(pl.multiple_of(tt * FEAT + i * 64, 64), 64), :] = quantized(x, top, w_peak).reshape(64, SUB)

    def unit_a(d, t):
        return w_all.at[d, pl.ds(pl.multiple_of(t * FEAT, 16), RA)]

    def unit_b(d, t):
        return w_all.at[d, pl.ds(pl.multiple_of(t * FEAT + RA, 16), FEAT - RA)]

    def bundle_b(t):
        return w_all.at[:, pl.ds(pl.multiple_of(t * FEAT + RA, 16), FEAT - RA)]

    rel = (0, -1, 1, -2, 2, -3, 3, -4)
    up = {0: 0, 1: 1, 2: 3, 3: 5, 4: 7}
    down = {0: 0, 1: 2, 2: 4, 3: 6}
    x_left, x_right, x_far, b_up, b_down, a_up, a_down = {}, {}, {}, {}, {}, {}, {}

    def x_sends(j):
        t_j = zt(rel[j])
        own = unit_a(dd, t_j)
        x_left[j] = copies.start(own, own, {"dp": xd(1)}, unit_a(xd(-1), t_j))
        x_right[j] = copies.start(own, own, {"dp": xd(-1)}, unit_a(xd(1), t_j))

    def a_send_up(step):
        u = unit_a(dd, zt(-step))
        a_up[step + 1] = copies.start(u, u, {"tp": zt(1)}, unit_a(dd, zt(-step - 1)))

    def a_send_down(step):
        u = unit_a(dd, zt(step))
        a_down[step + 1] = copies.start(u, u, {"tp": zt(-1)}, unit_a(dd, zt(step + 1)))

    def b_send_up(step):
        u = bundle_b(zt(-step))
        b_up[step + 1] = copies.start(u, u, {"tp": zt(1)}, bundle_b(zt(-step - 1)))

    def b_send_down(step):
        u = bundle_b(zt(step))
        b_down[step + 1] = copies.start(u, u, {"tp": zt(-1)}, bundle_b(zt(step + 1)))

    own_b = unit_b(dd, tt)
    bx_left = copies.start(own_b, own_b, {"dp": xd(1)}, unit_b(xd(-1), tt))
    bx_right = copies.start(own_b, own_b, {"dp": xd(-1)}, unit_b(xd(1), tt))
    a_send_up(0)
    a_send_down(0)
    x_sends(0)

    bx_far = []

    def ev_bx():
        bx_left.wait_recv()
        u = unit_b(xd(-1), tt)
        bx_far.append(copies.start(u, u, {"dp": xd(1)}, unit_b(xd(2), tt)))
        bx_right.wait_recv()

    def ev_b0():
        bx_far[0].wait_recv()
        b_send_up(0)
        b_send_down(0)

    def ev_a(step):
        def go():
            a_up[step].wait_recv()
            if step < 4:
                a_send_up(step)
            x_sends(up[step])
            if step < 4:
                a_down[step].wait_recv()
                if step < 3:
                    a_send_down(step)
                x_sends(down[step])

        return go

    def ev_b(step):
        def go():
            b_up[step].wait_recv()
            if step < 4:
                b_send_up(step)
            if step < 4:
                b_down[step].wait_recv()
                if step < 3:
                    b_send_down(step)

        return go

    def ev_x(j):
        def go():
            t_j = zt(rel[j])
            x_left[j].wait_recv()
            if j % 2 == 0:
                u = unit_a(xd(-1), t_j)
                x_far[j] = copies.start(u, u, {"dp": xd(1)}, unit_a(xd(2), t_j))
            x_right[j].wait_recv()
            if j % 2 == 1:
                u = unit_a(xd(1), t_j)
                x_far[j] = copies.start(u, u, {"dp": xd(-1)}, unit_a(xd(2), t_j))

        return go

    events = [
        ev_bx,
        ev_a(1),
        ev_b0,
        ev_x(0),
        ev_a(2),
        ev_x(1),
        ev_b(1),
        ev_x(2),
        ev_a(3),
        ev_x(3),
        ev_b(2),
        ev_a(4),
        ev_x(4),
        ev_b(3),
        ev_x(5),
        ev_x(6),
        ev_b(4),
        ev_x(7),
    ]
    done = [0]

    def progress(upto):
        while done[0] < min(upto, len(events)):
            events[done[0]]()
            done[0] += 1

    kv.x0.wait_recv()
    attend_if_before(sid(0, 1))
    kv.low()
    attend_if_before(sid(-1, 0))
    kv.high()
    progress(1)
    attend_if_before(sid(1, 0))
    kv.x3.wait_recv()
    attend_if_before(sid(-1, 1))
    kv.far()
    progress(2)
    kv.x5.wait_recv()
    attend_if_before(sid(1, 1))
    progress(4)
    attend_if_before(sid(2, 0))
    kv.x7.wait_recv()
    progress(5)
    attend_if_before(sid(2, 1))

    tiles[49] = jnp.zeros((8, 128), F32)
    for h in range(HEADS):
        a = (o_ref[h] / l_ref[h]).T.astype(BF16)
        att_buf[:, h * HEAD : (h + 1) * HEAD] = a
        tiles[49] = jnp.maximum(tiles[49], jnp.max(jnp.abs(a.astype(F32)).reshape(TOK // 8, 8, HEAD), axis=0))
    tiles[16 + tt] = tiles[49]
    a_moves = []
    for k in range(1, NTP):
        a_moves.append(
            copies.start(
                att_buf.at[pl.ds(pl.multiple_of(zt(k) * OWN, OWN), OWN)],
                z_buf.at[tt],
                {"tp": zt(k)},
                z_buf.at[zt(-k)],
            )
        )
    a_top = spread_tile(49, 16, "tp", zt)
    z_buf[tt] = att_buf[pl.ds(pl.multiple_of(tt * OWN, OWN), OWN), :]
    progress(9)
    for cp in a_top:
        cp.wait_recv()
    tiles[50] = max_of_tiles(16)
    tiles[24 + ss] = tiles[50]
    s_top = spread_tile(50, 24, "seq", sq)
    for cp in a_moves:
        cp.wait_recv()
    for cp in s_top:
        cp.wait_recv()
    a_peak = jnp.max(max_of_tiles(24))

    @pl.loop(0, NTP)
    def _(i):
        for n in range(FEAT // 128):
            x = z_buf[i, :, n * 128 : (n + 1) * 128].astype(F32)
            cols = pl.ds(pl.multiple_of(i * FEAT + n * 128, 128), 128)
            act_all[ss, :, cols] = quantized(x, lane_block_max(jnp.abs(x)), a_peak)

    act = SeqGather(lambda i: act_all.at[i], lambda i, h: act_all.at[i, pl.ds(h * (OWN // 2), OWN // 2)])
    progress(12)
    act.low()
    act.high()
    progress(14)
    act.x0.wait_recv()
    act.far()
    act.x3.wait_recv()
    act.x5.wait_recv()
    act.x7.wait_recv()
    progress(len(events))

    moves = []

    def project(d, last):
        lhs = act_all[...].reshape(NSEQ * OWN, NTP * FEAT)
        prod = jnp.dot(lhs, w_all[d], preferred_element_type=F32)
        out_buf[d] = prod.astype(BF16).reshape(NSEQ, OWN, SUB)
        for k in range(1, NSEQ):
            moves.append(
                copies.start(
                    out_buf.at[d, sq(k)], part_buf.at[ss, d], {"seq": sq(k)}, part_buf.at[sq(-k), d]
                )
            )
        part_buf[ss, d] = out_buf[d, ss]

    project(dd, False)
    project(xd(-1), False)
    project(xd(1), False)
    for j in range(8):
        x_far[j].wait_recv()
    project(xd(2), True)
    loads[8].wait()
    for cp in moves:
        cp.wait_recv()

    square = jnp.zeros((OWN, 128), F32)
    for i in range(NSEQ):
        for j in range(NDP):
            cols = slice(i * COLS + j * SUB, i * COLS + (j + 1) * SUB)
            hid = res_buf[:, cols].astype(F32) + part_buf[i, j].astype(F32)
            hid_buf[:, cols] = hid
            new_ref[:, cols] = hid.astype(BF16)
            sqr = hid * hid
            for n in range(SUB // 128):
                square = square + sqr[:, n * 128 : (n + 1) * 128]
    mean = jnp.sum(square, axis=1, keepdims=True) * (1.0 / D)
    root = lax.rsqrt(mean + 1e-05)
    top = jnp.zeros((OWN, 128), F32)
    for i in range(D // 128):
        cols = slice(i * 128, (i + 1) * 128)
        normed = hid_buf[:, cols] * root * gain_ref[:, cols].astype(F32)
        hid_buf[:, cols] = normed
        top = jnp.maximum(top, jnp.abs(normed))
    tiles[51] = jnp.max(top.reshape(OWN // 8, 8, 128), axis=0)
    tiles[32 + tt] = tiles[51]
    for cp in spread_tile(51, 32, "tp", zt):
        cp.wait_recv()
    tiles[52] = max_of_tiles(32)
    tiles[40 + ss] = tiles[52]
    for cp in spread_tile(52, 40, "seq", sq):
        cp.wait_recv()
    n_peak = jnp.max(max_of_tiles(40))

    @pl.loop(0, D // 256)
    def _(i):
        for n in range(2):
            cols = pl.ds(pl.multiple_of(i * 256 + n * 128, 128), 128)
            x = hid_buf[:, cols]
            next_ref[:, cols] = quantized(x, lane_block_max(jnp.abs(x)), n_peak)

    copies.finish()


def local(queries, keys, values, out_weight, residual, norm_gain):
    any_space = pl.BlockSpec(memory_space=pl.ANY)
    vmem = pl.BlockSpec(memory_space=pltpu.VMEM)
    out = jax.ShapeDtypeStruct((OWN, D), BF16)
    return pl.pallas_call(
        kernel,
        out_shape=(out, out),
        in_specs=[any_space] * 5 + [vmem],
        out_specs=(vmem, vmem),
        scratch_shapes=[
            pltpu.VMEM((TOK, FEAT), BF16),
            pltpu.VMEM((NSEQ, 2, TOK, HEAD), BF16),
            pltpu.VMEM((FEAT, D), BF16),
            pltpu.VMEM((FEAT, SUB), BF16),
            pltpu.VMEM((NDP, NTP * FEAT, SUB), BF16),
            pltpu.VMEM((HEAD, TOK), BF16),
            pltpu.VMEM((HEADS, 1, TOK), F32),
            pltpu.VMEM((HEADS, 1, TOK), F32),
            pltpu.VMEM((HEADS, HEAD, TOK), F32),
            pltpu.VMEM((TOK, FEAT), BF16),
            pltpu.VMEM((NTP, OWN, FEAT), BF16),
            pltpu.VMEM((NSEQ, OWN, NTP * FEAT), BF16),
            pltpu.VMEM((NDP, NSEQ, OWN, SUB), BF16),
            pltpu.VMEM((NSEQ, NDP, OWN, SUB), BF16),
            pltpu.VMEM((OWN, D), BF16),
            pltpu.VMEM((OWN, D), F32),
            pltpu.VMEM((56, 8, 128), F32),
            pltpu.SemaphoreType.DMA((N_COPIES,)),
            pltpu.SemaphoreType.DMA((N_COPIES,)),
            pltpu.SemaphoreType.DMA((9,)),
        ],
        compiler_params=pltpu.CompilerParams(
            collective_id=0, has_side_effects=True, vmem_limit_bytes=60 * 1024 * 1024
        ),
    )(queries, keys, values, out_weight, residual, norm_gain.reshape(1, D))


def solution(mesh):
    in_specs = (
        P(("dp", "seq"), "tp"),
        P(("dp", "seq"), "tp"),
        P(("dp", "seq"), "tp"),
        P("tp", None),
        P(("dp", "seq", "tp"), None),
        P(),
    )
    out_specs = (P(("dp", "seq", "tp"), None), P(("dp", "seq", "tp"), None))
    return jax.shard_map(local, mesh=mesh, in_specs=in_specs, out_specs=out_specs, check_vma=False)
```

time: 339 us -> 146 us (0.43)
  Pallas kernels: 0 us -> 139 us
  other arithmetic: 130 us -> 0 us
  waiting for transfers between devices: 111 us -> 0 us
  matrix products: 41.2 us -> 0 us
  starting transfers between devices: 24.7 us -> 0 us
  between operations: 18.2 us -> 0.64 us
  local copies, waits for them, and re-layouts: 12.6 us -> 5.87 us
    pallas_call x0 -> x1, Pallas kernels: none -> 139 us  [local(): pl.pallas_call(kernel, out_shape=(out, out), in_specs=[any_space] * 5 + [...]
    reduce_scatter x1 -> x0, waiting for transfers between devices: 89.7 us -> none  [local(): lax.psum_scatter(lax.dot_general(act_q, weight_q, (((0,), (0,)), ((), ())...]
    convert_element_type x8 -> x0, other arithmetic: 81.2 us -> none  [the longest x3 79.4 us: fake_quant(): payload = soft_grid(blocks / spacing).astype(jnp.bfloat16)]
    dot_general x3 -> x0, matrix products: 41.2 us -> none  [the longest x1 16.7 us: attend_piece(): jnp.einsum('kgts,skd->kgtd', weights.astype(jnp.bfloat16), values_split,...]
    reduce_max x8 -> x0, other arithmetic: 27.9 us -> none  [the longest x3 16.8 us: fake_quant(): block_max = jnp.max(jnp.abs(blocks), axis=block_axis, keepdims=True)]
    all_to_all x3 -> x0, starting transfers between devices: 24.6 us -> none  [copy_for_each(): lax.all_to_all(jnp.broadcast_to(value[None], (devices, *value.shape)), ax...]
    all_to_all x3 -> x0, waiting for transfers between devices: 21.3 us -> none  [copy_for_each(): lax.all_to_all(jnp.broadcast_to(value[None], (devices, *value.shape)), ax...]
    reduce_sum x2 -> x0, other arithmetic: 16.8 us -> none  [the longest x1 15.2 us: attend_piece(): running_total = running_total * shrink_factor + jnp.sum(weights, axis=3)]
  transfers between devices with their start and end apart: 4 -> 0, of which waited for: 4 -> 0; matrix products, arithmetic and copies ran while one was open for 7% -> 0% of each run, Pallas kernels for 0% -> 0%
where the time goes in v1:
time: 146 us
  Pallas kernels  139 us (95%)
  local copies, waits for them, and re-layouts  5.87 us (4%)
    pallas_call x1, Pallas kernels, local(): pl.pallas_call(kernel, out_shape=(out, out), in_specs=[any_space] * 5 + [...  139 us
    unnamed x2, local copies, waits for them, and re-layouts  4.52 us

profile of v1, /device:TPU:1, one launch (start us, length us, event | category | flops | bytes accessed | tf_op | source)
XLA Modules:
  0.0 145.9 jit_solution(3659052570877749021)
XLA Ops:
  0.6 1.4 reshape.7.gain_ref
  2.0 139.4 %shard_map.77 = (bf16[64,8192]{1,0:T(8,128)(2,1)}, bf16[64,8192]{1,0:T(8,128)(2,1)}) custom-call(bf16[512,512]{1,0:T(8,128)(2,1)} %q_hbm.1, bf16[512,128]{1,0:T(8,128)(2,1)} %k_hbm.1, bf16[512,128]{1,0:T(8,128)(2,1)} %v_hbm.1, bf16[512,8192]{1,0:T(8,128)(2,1)} %w_hbm.1, bf16[64,8192]{1,0:T(8,128)(2,1)} %res_hbm.1, bf16[1,8192]{1,0:T(2,128)(2,1)} %reshape.7.gain_ref), custom_call_target="tpu_custom_call" | custom-call | tf_op jit(solution)/shard_map/pallas_call | solution.py:543
  141.4 2.3 %copy.10 = bf16[64,8192]{1,0:T(8,128)(2,1)} copy(bf16[64,8192]{1,0:T(8,128)(2,1)} %get-tuple-element.4) | data formatting | bytes 2097152
  143.7 2.3 %copy.11 = bf16[64,8192]{1,0:T(8,128)(2,1)} copy(bf16[64,8192]{1,0:T(8,128)(2,1)} %get-tuple-element.5) | data formatting | bytes 2097152

commit v2 on v1

v2 whole, which is shorter than its diff:
```python
import jax
import jax.numpy as jnp
from jax import lax
from jax.experimental import pallas as pl
from jax.experimental.pallas import tpu as pltpu
from jax.sharding import PartitionSpec as P

D = 8192
HEAD = 128
FLOOR = 256.0
NEG = -1e30
MESH = pl.DeviceIdType.MESH
F32 = jnp.float32
BF16 = jnp.bfloat16

TOK = 512
HEADS = 4
FEAT = HEADS * HEAD
NTP = 8
NSEQ = 8
NDP = 4
OWN = TOK // NTP
COLS = D // NSEQ
SUB = COLS // NDP
PAIR = 2
HALF = OWN // 2
GROUP = 2
RA = 432
SCALE = HEAD ** (-0.5) * 1.4426950408889634

SINE = (
    -1.7606472969055176,
    5.904375076293945,
    -10.969871520996094,
    11.68786334991455,
    -5.921726226806641,
    0.8999996781349182,
)


def rounded(x, double):
    v = x / double
    f = v - jnp.round(v)
    z = f * f
    sine = SINE[0] * z + SINE[1]
    for co in SINE[2:]:
        sine = sine * z + co
    half = (v - f * sine).astype(BF16).astype(F32)
    return (half * double).astype(BF16)


def quantized_rows(x, peak):
    n, cols = x.shape
    x = x.reshape(n // 16, 16, cols)
    top = jnp.max(jnp.abs(x), axis=1, keepdims=True)
    tensor_scale = peak / (6.0 * 448.0)
    scale = jnp.maximum(top * (1.0 / (6.0 * tensor_scale)), FLOOR).astype(BF16).astype(F32)
    return rounded(x, jnp.broadcast_to(scale * (2.0 * tensor_scale), x.shape)).reshape(n, cols)


def quantized_lanes(pieces, peak, pick):
    rows = pieces[0].shape[0]
    tensor_scale = peak / (6.0 * 448.0)
    inverse = 1.0 / (6.0 * tensor_scale)
    scales = []
    for x in pieces:
        top = jnp.abs(x)
        for sh in (1, 2, 4, 8):
            top = jnp.maximum(top, pltpu.roll(top, sh, 1))
        scales.append(jnp.maximum(top * inverse, FLOOR).astype(BF16))
    spread = jnp.dot(jnp.concatenate(scales, axis=0), pick, preferred_element_type=F32)
    return [
        rounded(x, spread[i * rows : (i + 1) * rows] * (2.0 * tensor_scale)) for i, x in enumerate(pieces)
    ]


def pick_matrix():
    src = lax.broadcasted_iota(jnp.int32, (128, 128), 0)
    dst = lax.broadcasted_iota(jnp.int32, (128, 128), 1)
    same = (src // 16 == dst // 16) & (src % 16 == 15)
    return jnp.where(same, 1.0, 0.0).astype(BF16)


class Copies:
    def __init__(self, send_sems, recv_sems, dev):
        self.send_sems, self.recv_sems, self.dev = send_sems, recv_sems, dev
        self.sent, self.n_recv = [], 0

    def copy(self, src, dst, send, recv, dev):
        return pltpu.make_async_remote_copy(
            src_ref=src,
            dst_ref=dst,
            send_sem=self.send_sems.at[send],
            recv_sem=self.recv_sems.at[recv],
            device_id=dev,
            device_id_type=MESH,
        )

    def sender(self, total):
        self.sent.append(total)
        return len(self.sent) - 1

    def receiver(self):
        self.n_recv += 1
        return self.n_recv - 1

    def start(self, src, dst, dev, send, recv):
        self.copy(src, dst, send, recv, dev).start()

    def start_one(self, src, dst, dev, send, landing):
        recv = self.receiver()
        self.start(src, dst, dev, send, recv)
        return lambda: self.arrived(recv, landing)

    def arrived(self, recv, landing):
        self.copy(landing, landing, 0, recv, self.dev).wait_recv()

    def finish(self):
        for i, total in enumerate(self.sent):
            self.copy(total, total, i, 0, self.dev).wait_send()


N_SEND = 12
N_RECV = 73


def kernel(
    q_hbm,
    k_hbm,
    v_hbm,
    w_hbm,
    res_hbm,
    gain_ref,
    hid_ref,
    root_ref,
    top_ref,
    q_buf,
    kv_buf,
    w_stage,
    w_slice,
    w_all,
    vt_buf,
    m_ref,
    l_ref,
    o_ref,
    att_buf,
    z_buf,
    act_all,
    out_buf,
    part_buf,
    res_buf,
    hid_buf,
    tiles,
    pick_buf,
    root_buf,
    send_sems,
    recv_sems,
    local_sems,
):
    dd, ss, tt = lax.axis_index("dp"), lax.axis_index("seq"), lax.axis_index("tp")
    yy = lax.div(ss, 2)
    cc = ss - 2 * yy

    def sid(dy, dc):
        return lax.rem(yy + dy + 4, 4) * 2 + (cc if dc == 0 else 1 - cc)

    def zt(k):
        return lax.rem(tt + k + 2 * NTP, NTP)

    def sq(k):
        return lax.rem(ss + k + 2 * NSEQ, NSEQ)

    def xd(k):
        return lax.rem(dd + k + 2 * NDP, NDP)

    loads = [
        pltpu.make_async_copy(k_hbm, kv_buf.at[ss, 0], local_sems.at[0]),
        pltpu.make_async_copy(v_hbm, kv_buf.at[ss, 1], local_sems.at[1]),
        pltpu.make_async_copy(q_hbm, q_buf, local_sems.at[2]),
        pltpu.make_async_copy(
            w_hbm.at[:, pl.ds(pl.multiple_of(ss * COLS + dd * SUB, SUB), SUB)],
            w_slice,
            local_sems.at[3],
        ),
    ]
    for i in range(4):
        loads.append(
            pltpu.make_async_copy(
                w_hbm.at[pl.ds(i * 128, 128)], w_stage.at[pl.ds(i * 128, 128)], local_sems.at[4 + i]
            )
        )
    loads.append(pltpu.make_async_copy(res_hbm, res_buf, local_sems.at[8]))
    for load in loads:
        load.start()

    barrier = pltpu.get_barrier_semaphore()
    for k in range(1, NTP):
        pl.semaphore_signal(barrier, inc=1, device_id={"tp": zt(k)}, device_id_type=MESH)
    for k in range(1, NSEQ):
        pl.semaphore_signal(barrier, inc=1, device_id={"seq": sq(k)}, device_id_type=MESH)
    for k in (1, 3):
        pl.semaphore_signal(barrier, inc=1, device_id={"dp": xd(k)}, device_id_type=MESH)
    pl.semaphore_wait(barrier, NTP - 1 + NSEQ - 1 + 2)

    copies = Copies(send_sems, recv_sems, {"tp": zt(1)})
    pick_buf[...] = pick_matrix()

    class SeqGather:
        def __init__(self, unit, half, total):
            self.unit, self.half, self.send = unit, half, copies.sender(total)
            own = unit(sid(0, 0))
            self.x1 = self.go(own, sid(1, 0), unit(sid(-1, 0)))
            self.x2 = self.go(own, sid(-1, 0), unit(sid(1, 0)))
            self.x0 = self.go(own, sid(0, 1), unit(sid(0, 1)))

        def go(self, ref, to, landing):
            return copies.start_one(ref, ref, {"seq": to}, self.send, landing)

        def low(self):
            self.x1()
            got, part = self.unit(sid(-1, 0)), self.half(sid(-1, 0), 0)
            self.x4 = self.go(part, sid(1, 0), self.half(sid(2, 0), 0))
            self.x3 = self.go(got, sid(0, 1), self.unit(sid(-1, 1)))

        def high(self):
            self.x2()
            got, part = self.unit(sid(1, 0)), self.half(sid(1, 0), 1)
            self.x6 = self.go(part, sid(-1, 0), self.half(sid(2, 0), 1))
            self.x5 = self.go(got, sid(0, 1), self.unit(sid(1, 1)))

        def far(self):
            self.x4()
            self.x6()
            self.x7 = self.go(self.unit(sid(2, 0)), sid(0, 1), self.unit(sid(2, 1)))

    def spread_tile(src, dst_of, axis, at):
        me = tt if axis == "tp" else ss
        seven = tiles.at[pl.ds(dst_of, 7)]
        send, recv = copies.sender(seven), copies.receiver()
        for k in range(1, 8):
            copies.start(tiles.at[src], tiles.at[dst_of + me], {axis: at(k)}, send, recv)
        return lambda: copies.arrived(recv, seven)

    def max_of_tiles(first):
        top = tiles[first]
        for i in range(1, 8):
            top = jnp.maximum(top, tiles[first + i])
        return top

    loads[0].wait()
    loads[1].wait()
    kv = SeqGather(lambda i: kv_buf.at[i], lambda i, h: kv_buf.at[i, h], kv_buf.at[pl.ds(0, NSEQ - 1)])

    tiles[48] = jnp.zeros((8, 128), F32)
    for i in range(4):
        loads[4 + i].wait()

        @pl.loop(0, 16)
        def _(j, i=i):
            top = tiles[48]
            piece = jnp.abs(w_stage[i * 128 : (i + 1) * 128, pl.ds(pl.multiple_of(j * 512, 512), 512)].astype(F32))
            top4 = jnp.max(piece.reshape(16, 8, 512), axis=0)
            for n in range(4):
                top = jnp.maximum(top, top4[:, n * 128 : (n + 1) * 128])
            tiles[48] = top

    tiles[8 + tt] = tiles[48]
    w_top = spread_tile(48, 8, "tp", zt)

    def attend(block, kind):
        vt_buf[...] = kv_buf[block, 1].T

        @pl.loop(0, HEADS // PAIR)
        def _(i):
            heads = [i * PAIR + n for n in range(PAIR)]
            scores = [
                lax.dot_general(
                    kv_buf[block, 0],
                    q_buf[:, pl.ds(pl.multiple_of(h * HEAD, HEAD), HEAD)],
                    (((1,), (1,)), ((), ())),
                    preferred_element_type=F32,
                )
                for h in heads
            ]
            for h, sc in zip(heads, scores):
                if kind == "own":
                    key = lax.broadcasted_iota(jnp.int32, (TOK, TOK), 0)
                    query = lax.broadcasted_iota(jnp.int32, (TOK, TOK), 1)
                    sc = jnp.where(key <= query, sc, NEG)
                top = jnp.max(sc, axis=0, keepdims=True)
                if kind != "own":
                    old = m_ref[h]
                    top = jnp.maximum(old, top)
                p = jnp.exp2((sc - top) * SCALE)
                total = jnp.sum(p, axis=0, keepdims=True)
                o = lax.dot_general(
                    vt_buf[...], p.astype(BF16), (((1,), (0,)), ((), ())), preferred_element_type=F32
                )
                if kind != "own":
                    shrink = jnp.exp2((old - top) * SCALE)
                    total = total + l_ref[h] * shrink
                    o = o + o_ref[h] * shrink
                m_ref[h] = top
                l_ref[h] = total
                o_ref[h] = o

    def attend_if_before(block):
        @pl.when(block < ss)
        def _():
            attend(block, "before")

    loads[2].wait()
    attend(ss, "own")

    loads[3].wait()
    w_top()
    w_peak = jnp.max(max_of_tiles(8))

    @pl.loop(0, 8)
    def _(i):
        rows = pl.ds(pl.multiple_of(i * 64, 64), 64)
        w_all[dd, pl.ds(pl.multiple_of(tt * FEAT + i * 64, 64), 64), :] = quantized_rows(
            w_slice[rows, :].astype(F32), w_peak
        )

    def unit_a(d, t):
        return w_all.at[d, pl.ds(pl.multiple_of(t * FEAT, 16), RA)]

    def unit_b(d, t):
        return w_all.at[d, pl.ds(pl.multiple_of(t * FEAT + RA, 16), FEAT - RA)]

    def bundle_b(t):
        return w_all.at[:, pl.ds(pl.multiple_of(t * FEAT + RA, 16), FEAT - RA)]

    rel = (0, -1, 1, -2, 2, -3, 3, -4)
    up = {0: 0, 1: 1, 2: 3, 3: 5, 4: 7}
    down = {0: 0, 1: 2, 2: 4, 3: 6}
    x_left, x_right, x_far, b_up, b_down, a_up, a_down = {}, {}, {}, {}, {}, {}, {}

    w_send = copies.sender(w_all.at[:, pl.ds(0, 31 * FEAT // NDP)])

    def w_go(ref, to, landing):
        return copies.start_one(ref, ref, to, w_send, landing)

    def x_sends(j):
        t_j = zt(rel[j])
        own = unit_a(dd, t_j)
        x_left[j] = w_go(own, {"dp": xd(1)}, unit_a(xd(-1), t_j))
        x_right[j] = w_go(own, {"dp": xd(-1)}, unit_a(xd(1), t_j))

    def a_send_up(step):
        a_up[step + 1] = w_go(unit_a(dd, zt(-step)), {"tp": zt(1)}, unit_a(dd, zt(-step - 1)))

    def a_send_down(step):
        a_down[step + 1] = w_go(unit_a(dd, zt(step)), {"tp": zt(-1)}, unit_a(dd, zt(step + 1)))

    def b_send_up(step):
        b_up[step + 1] = w_go(bundle_b(zt(-step)), {"tp": zt(1)}, bundle_b(zt(-step - 1)))

    def b_send_down(step):
        b_down[step + 1] = w_go(bundle_b(zt(step)), {"tp": zt(-1)}, bundle_b(zt(step + 1)))

    own_b = unit_b(dd, tt)
    bx_left = w_go(own_b, {"dp": xd(1)}, unit_b(xd(-1), tt))
    bx_right = w_go(own_b, {"dp": xd(-1)}, unit_b(xd(1), tt))
    a_send_up(0)
    a_send_down(0)
    x_sends(0)

    bx_far = []

    def ev_bx():
        bx_left()
        bx_far.append(w_go(unit_b(xd(-1), tt), {"dp": xd(1)}, unit_b(xd(2), tt)))
        bx_right()

    def ev_b0():
        bx_far[0]()
        b_send_up(0)
        b_send_down(0)

    def ev_a(step):
        def go():
            a_up[step]()
            if step < 4:
                a_send_up(step)
            x_sends(up[step])
            if step < 4:
                a_down[step]()
                if step < 3:
                    a_send_down(step)
                x_sends(down[step])

        return go

    def ev_b(step):
        def go():
            b_up[step]()
            if step < 4:
                b_send_up(step)
                b_down[step]()
                if step < 3:
                    b_send_down(step)

        return go

    def ev_x(j):
        def go():
            t_j = zt(rel[j])
            x_left[j]()
            if j % 2 == 0:
                x_far[j] = w_go(unit_a(xd(-1), t_j), {"dp": xd(1)}, unit_a(xd(2), t_j))
            x_right[j]()
            if j % 2 == 1:
                x_far[j] = w_go(unit_a(xd(1), t_j), {"dp": xd(-1)}, unit_a(xd(2), t_j))

        return go

    events = [
        ev_bx,
        ev_a(1),
        ev_x(0),
        ev_b0,
        ev_a(2),
        ev_x(1),
        ev_x(2),
        ev_b(1),
        ev_a(3),
        ev_x(3),
        ev_b(2),
        ev_a(4),
        ev_x(4),
        ev_x(5),
        ev_b(3),
        ev_x(6),
        ev_x(7),
        ev_b(4),
    ]
    done = [0]

    def progress(upto):
        while done[0] < min(upto, len(events)):
            events[done[0]]()
            done[0] += 1

    kv.x0()
    attend_if_before(sid(0, 1))
    kv.low()
    attend_if_before(sid(-1, 0))
    kv.high()
    progress(2)
    attend_if_before(sid(1, 0))
    kv.x3()
    progress(4)
    attend_if_before(sid(-1, 1))
    kv.far()
    progress(5)
    kv.x5()
    attend_if_before(sid(1, 1))
    progress(6)
    attend_if_before(sid(2, 0))
    kv.x7()
    progress(8)
    attend_if_before(sid(2, 1))

    tiles[49] = jnp.zeros((8, 128), F32)
    for h in range(HEADS):
        a = (o_ref[h] / l_ref[h]).T.astype(BF16)
        att_buf[:, h * HEAD : (h + 1) * HEAD] = a
        tiles[49] = jnp.maximum(tiles[49], jnp.max(jnp.abs(a.astype(F32)).reshape(TOK // 8, 8, HEAD), axis=0))
    tiles[16 + tt] = tiles[49]
    a_top = spread_tile(49, 16, "tp", zt)
    a_moves = []
    for part in range(2):
        seven = z_buf.at[part, pl.ds(0, NTP - 1)]
        send, recv = copies.sender(seven), copies.receiver()
        for k in range(1, NTP):
            copies.start(
                att_buf.at[pl.ds(pl.multiple_of(zt(k) * OWN + part * HALF, HALF), HALF)],
                z_buf.at[part, tt],
                {"tp": zt(k)},
                send,
                recv,
            )
        a_moves.append(lambda recv=recv, seven=seven: copies.arrived(recv, seven))
        z_buf[part, tt] = att_buf[pl.ds(pl.multiple_of(tt * OWN + part * HALF, HALF), HALF), :]
    progress(10)
    a_top()
    tiles[50] = max_of_tiles(16)
    tiles[24 + ss] = tiles[50]
    s_top = spread_tile(50, 24, "seq", sq)
    progress(12)
    s_top()
    a_peak = jnp.max(max_of_tiles(24))

    acts = []
    for part in range(2):
        a_moves[part]()

        @pl.loop(0, NTP // GROUP)
        def _(i, part=part):
            pieces = [
                z_buf[part, GROUP * i + g, :, n * 128 : (n + 1) * 128].astype(F32)
                for g in range(GROUP)
                for n in range(FEAT // 128)
            ]
            for n, x in enumerate(quantized_lanes(pieces, a_peak, pick_buf[...])):
                act_all[ss, part, :, pl.ds(pl.multiple_of(i * GROUP * FEAT + n * 128, 128), 128)] = x

        acts.append(
            SeqGather(
                lambda i, part=part: act_all.at[i, part],
                lambda i, h, part=part: act_all.at[i, part, pl.ds(h * (HALF // 2), HALF // 2)],
                act_all.at[pl.ds(0, NSEQ - 1), part],
            )
        )
        progress(13 + 2 * part)

    part_seven = part_buf.at[pl.ds(0, NSEQ - 1)]
    out_send, out_recv = copies.sender(part_seven), copies.receiver()

    def sub_of(i):
        return lax.rem(dd + i + lax.div(i, 2) - 2 * lax.div(i, 3), NDP)

    def project(dy, first, count):
        chip = lax.rem(yy + dy + 4, 4)

        @pl.loop(first, first + count)
        def _(i):
            lhs = act_all[pl.ds(chip * 2, 2)].reshape(2 * OWN, NTP * FEAT)
            prod = jnp.dot(lhs, w_all[sub_of(i)], preferred_element_type=F32).astype(BF16)
            out_buf[chip * 2, i] = prod[:OWN]
            out_buf[chip * 2 + 1, i] = prod[OWN:]

        subs = pl.ds(first, count)
        for dc in range(2):
            to = sid(dy, dc)
            if dy == 0 and dc == 0:
                part_buf[ss, first : first + count] = out_buf[ss, first : first + count]
            else:
                copies.start(out_buf.at[to, subs], part_buf.at[ss, subs], {"seq": to}, out_send, out_recv)

    acts[0].low()
    acts[0].high()
    progress(16)
    acts[1].low()
    acts[1].high()
    progress(17)
    acts[0].far()
    progress(len(events))
    for a in acts:
        a.x0()
    project(0, 0, 3)
    acts[1].far()
    for a in acts:
        a.x3()
    project(-1, 0, 3)
    for a in acts:
        a.x5()
    project(1, 0, 3)
    for a in acts:
        a.x7()
    project(2, 0, 3)
    for j in range(8):
        x_far[j]()
    for dy in (2, -1, 1, 0):
        project(dy, 3, 1)
    loads[8].wait()
    copies.arrived(out_recv, part_seven)

    square = jnp.zeros((OWN, 128), F32)
    for i in range(NSEQ):
        for j in range(NDP):
            cols = pl.ds(pl.multiple_of(i * COLS + sub_of(j) * SUB, SUB), SUB)
            hid = res_buf[:, cols].astype(F32) + part_buf[i, j].astype(F32)
            hid_buf[:, cols] = hid
            sqr = hid * hid
            for n in range(SUB // 128):
                square = square + sqr[:, n * 128 : (n + 1) * 128]
    store = pltpu.make_async_copy(hid_buf, hid_ref, local_sems.at[9])
    store.start()
    mean = jnp.sum(square, axis=1, keepdims=True) * (1.0 / D)
    root = jnp.broadcast_to(lax.rsqrt(mean + 1e-05), (OWN, 128))
    root_buf[...] = root
    store_root = pltpu.make_async_copy(root_buf, root_ref, local_sems.at[10])
    store_root.start()
    top = jnp.zeros((OWN, 128), F32)
    for i in range(D // 128):
        top = jnp.maximum(top, jnp.abs(hid_buf[:, i * 128 : (i + 1) * 128] * root * gain_ref[i : i + 1, :].astype(F32)))
    tiles[51] = jnp.max(top.reshape(OWN // 8, 8, 128), axis=0)
    tiles[32 + tt] = tiles[51]
    spread_tile(51, 32, "tp", zt)()
    tiles[52] = max_of_tiles(32)
    tiles[40 + ss] = tiles[52]
    spread_tile(52, 40, "seq", sq)()
    tiles[53] = max_of_tiles(40)
    store_top = pltpu.make_async_copy(tiles.at[53], top_ref, local_sems.at[11])
    store_top.start()

    assert len(copies.sent) == N_SEND and copies.n_recv == N_RECV
    copies.finish()
    store.wait()
    store_root.wait()
    store_top.wait()


STEPS = 4
TILES = 8


def quantize_kernel(hid_ref, root_ref, gain_ref, top_ref, new_ref, next_ref):
    peak = jnp.max(top_ref[...])
    pick = pick_matrix()
    root = root_ref[...]

    @pl.loop(0, D // STEPS // 128 // TILES)
    def _(i):
        pieces, cols = [], []
        for n in range(TILES):
            cols.append(pl.ds(pl.multiple_of((i * TILES + n) * 128, 128), 128))
            hid = hid_ref[:, cols[n]]
            new_ref[:, cols[n]] = hid.astype(BF16)
            gain = gain_ref[pl.ds(i * TILES + n, 1), :].astype(F32)
            pieces.append(hid * root * gain)
        for n, x in enumerate(quantized_lanes(pieces, peak, pick)):
            next_ref[:, cols[n]] = x


def local(queries, keys, values, out_weight, residual, norm_gain):
    any_space = pl.BlockSpec(memory_space=pl.ANY)
    vmem = pl.BlockSpec(memory_space=pltpu.VMEM)
    gain = norm_gain.reshape(D // 128, 128).astype(F32)
    hid, root, top = pl.pallas_call(
        kernel,
        out_shape=(
            jax.ShapeDtypeStruct((OWN, D), F32),
            jax.ShapeDtypeStruct((OWN, 128), F32),
            jax.ShapeDtypeStruct((8, 128), F32),
        ),
        in_specs=[any_space] * 5 + [vmem],
        out_specs=(any_space, any_space, any_space),
        scratch_shapes=[
            pltpu.VMEM((TOK, FEAT), BF16),
            pltpu.VMEM((NSEQ, 2, TOK, HEAD), BF16),
            pltpu.VMEM((FEAT, D), BF16),
            pltpu.VMEM((FEAT, SUB), BF16),
            pltpu.VMEM((NDP, NTP * FEAT, SUB), BF16),
            pltpu.VMEM((HEAD, TOK), BF16),
            pltpu.VMEM((HEADS, 1, TOK), F32),
            pltpu.VMEM((HEADS, 1, TOK), F32),
            pltpu.VMEM((HEADS, HEAD, TOK), F32),
            pltpu.VMEM((TOK, FEAT), BF16),
            pltpu.VMEM((2, NTP, HALF, FEAT), BF16),
            pltpu.VMEM((NSEQ, 2, HALF, NTP * FEAT), BF16),
            pltpu.VMEM((NSEQ, NDP, OWN, SUB), BF16),
            pltpu.VMEM((NSEQ, NDP, OWN, SUB), BF16),
            pltpu.VMEM((OWN, D), BF16),
            pltpu.VMEM((OWN, D), F32),
            pltpu.VMEM((56, 8, 128), F32),
            pltpu.VMEM((128, 128), BF16),
            pltpu.VMEM((OWN, 128), F32),
            pltpu.SemaphoreType.DMA((N_SEND,)),
            pltpu.SemaphoreType.DMA((N_RECV,)),
            pltpu.SemaphoreType.DMA((12,)),
        ],
        compiler_params=pltpu.CompilerParams(
            collective_id=0, has_side_effects=True, vmem_limit_bytes=60 * 1024 * 1024
        ),
    )(queries, keys, values, out_weight, residual, gain)
    out = jax.ShapeDtypeStruct((OWN, D), BF16)
    wide = pl.BlockSpec((OWN, D // STEPS), lambda i: (0, i))
    return pl.pallas_call(
        quantize_kernel,
        grid=(STEPS,),
        out_shape=(out, out),
        in_specs=[
            wide,
            pl.BlockSpec((OWN, 128), lambda i: (0, 0)),
            pl.BlockSpec((D // STEPS // 128, 128), lambda i: (i, 0)),
            pl.BlockSpec((8, 128), lambda i: (0, 0)),
        ],
        out_specs=(wide, wide),
    )(hid, root, gain, top)


def solution(mesh):
    in_specs = (
        P(("dp", "seq"), "tp"),
        P(("dp", "seq"), "tp"),
        P(("dp", "seq"), "tp"),
        P("tp", None),
        P(("dp", "seq", "tp"), None),
        P(),
    )
    out_specs = (P(("dp", "seq", "tp"), None), P(("dp", "seq", "tp"), None))
    return jax.shard_map(local, mesh=mesh, in_specs=in_specs, out_specs=out_specs, check_vma=False)
```

time: 146 us -> 112 us (0.77)
  Pallas kernels: 139 us -> 110 us
  local copies, waits for them, and re-layouts: 5.87 us -> 0 us
    pallas_call x1 -> x2, Pallas kernels: 139 us -> 110 us  [the longest x1 102 us: local(): pl.pallas_call(kernel, out_shape=(jax.ShapeDtypeStruct((OWN, D), F32), ja...]
    unnamed x2 -> x0, local copies, waits for them, and re-layouts: 4.52 us -> none
where the time goes in v2:
time: 112 us
  Pallas kernels  110 us (98%)
  other arithmetic  1.34 us (1%)
    pallas_call x1, Pallas kernels, local(): pl.pallas_call(kernel, out_shape=(jax.ShapeDtypeStruct((OWN, D), F32), ja...  102 us
    pallas_call x1, Pallas kernels, local(): pl.pallas_call(quantize_kernel, grid=(STEPS,), out_shape=(out, out), in_s...  7.37 us

profile of v2, /device:TPU:1, one launch (start us, length us, event | category | flops | bytes accessed | tf_op | source)
XLA Modules:
  0.0 111.7 jit_solution(9869142205886934274)
XLA Ops:
  0.6 1.3 %bitcast_convert_fusion.gain_ref = f32[64,128]{1,0:T(8,128)} fusion(bf16[8192]{0:T(1024)(128)(2,1)} %param.11), kind=kLoop, calls=%fused_computation | loop fusion | flops 8192 | bytes 49152 | tf_op jit(solution)/shard_map/convert_element_type | solution.py:632
  2.0 102.4 %shard_map.77 = (f32[64,8192]{1,0:T(8,128)}, f32[64,128]{1,0:T(8,128)}, f32[8,128]{1,0:T(8,128)}) custom-call(bf16[512,512]{1,0:T(8,128)(2,1)} %q_hbm.1, bf16[512,128]{1,0:T(8,128)(2,1)} %k_hbm.1, bf16[512,128]{1,0:T(8,128)(2,1)} %v_hbm.1, bf16[512,8192]{1,0:T(8,128)(2,1)} %w_hbm.1, bf16[64,8192]{1,0:T(8,128)(2,1)} %res_hbm.1, ...), custom_call_target="tpu_custom_call" | custom-call | tf_op jit(solution)/shard_map/pallas_call | solution.py:633
  104.3 7.4 %shard_map.78 = (bf16[64,8192]{1,0:T(8,128)(2,1)}, bf16[64,8192]{1,0:T(8,128)(2,1)}) custom-call(f32[64,8192]{1,0:T(8,128)} %get-tuple-element.5.hid_ref, f32[64,128]{1,0:T(8,128)} %get-tuple-element.6.root_ref, f32[64,128]{1,0:T(8,128)} %bitcast_convert_fusion.gain_ref, f32[8,128]{1,0:T(8,128)} %get-tuple-element.7.top_ref), custom_call_target="tpu_custom_call" | custom-call | tf_op jit(solution)/shard_map/pallas_call | solution.py:672

commit v3 on v2

--- a/solution.py
+++ b/solution.py
@@ -22,10 +22,10 @@
 OWN = TOK // NTP
 COLS = D // NSEQ
 SUB = COLS // NDP
-PAIR = 2
+PAIR = 4
 HALF = OWN // 2
 GROUP = 2
-RA = 432
+RA = 416
 SCALE = HEAD ** (-0.5) * 1.4426950408889634
 
 SINE = (
@@ -120,8 +120,8 @@
             self.copy(total, total, i, 0, self.dev).wait_send()
 
 
-N_SEND = 12
-N_RECV = 73
+N_SEND = 13
+N_RECV = 72
 
 
 def kernel(
@@ -137,7 +137,7 @@
     q_buf,
     kv_buf,
     w_stage,
-    w_slice,
+    w_raw,
     w_all,
     vt_buf,
     m_ref,
@@ -179,7 +179,7 @@
         pltpu.make_async_copy(q_hbm, q_buf, local_sems.at[2]),
         pltpu.make_async_copy(
             w_hbm.at[:, pl.ds(pl.multiple_of(ss * COLS + dd * SUB, SUB), SUB)],
-            w_slice,
+            w_raw.at[dd],
             local_sems.at[3],
         ),
     ]
@@ -200,7 +200,6 @@
         pl.semaphore_signal(barrier, inc=1, device_id={"seq": sq(k)}, device_id_type=MESH)
     for k in (1, 3):
         pl.semaphore_signal(barrier, inc=1, device_id={"dp": xd(k)}, device_id_type=MESH)
-    pl.semaphore_wait(barrier, NTP - 1 + NSEQ - 1 + 2)
 
     copies = Copies(send_sems, recv_sems, {"tp": zt(1)})
     pick_buf[...] = pick_matrix()
@@ -246,10 +245,6 @@
         for i in range(1, 8):
             top = jnp.maximum(top, tiles[first + i])
         return top
-
-    loads[0].wait()
-    loads[1].wait()
-    kv = SeqGather(lambda i: kv_buf.at[i], lambda i, h: kv_buf.at[i, h], kv_buf.at[pl.ds(0, NSEQ - 1)])
 
     tiles[48] = jnp.zeros((8, 128), F32)
     for i in range(4):
@@ -265,6 +260,30 @@
             tiles[48] = top
 
     tiles[8 + tt] = tiles[48]
+    pl.semaphore_wait(barrier, NTP - 1 + NSEQ - 1 + 2)
+    loads[0].wait()
+    loads[1].wait()
+    kv = SeqGather(lambda i: kv_buf.at[i], lambda i, h: kv_buf.at[i, h], kv_buf.at[pl.ds(0, NSEQ - 1)])
+
+    loads[3].wait()
+    raw_send = copies.sender(w_raw.at[pl.ds(0, NDP - 1)])
+    raw_far = []
+
+    def raw_go(ref, to, landing):
+        return copies.start_one(ref, ref, {"dp": to}, raw_send, landing)
+
+    raw_left = raw_go(w_raw.at[dd], xd(1), w_raw.at[xd(-1)])
+    raw_right = raw_go(w_raw.at[dd], xd(-1), w_raw.at[xd(1)])
+
+    def raw_forward():
+        for arrival, d, to, rows in (
+            (raw_left, xd(-1), xd(1), pl.ds(0, FEAT // 2)),
+            (raw_right, xd(1), xd(-1), pl.ds(FEAT // 2, FEAT // 2)),
+        ):
+            arrival()
+            raw_far.append(raw_go(w_raw.at[d, rows], to, w_raw.at[xd(2), rows]))
+
+
     w_top = spread_tile(48, 8, "tp", zt)
 
     def attend(block, kind):
@@ -312,22 +331,23 @@
     loads[2].wait()
     attend(ss, "own")
 
-    loads[3].wait()
     w_top()
     w_peak = jnp.max(max_of_tiles(8))
 
-    @pl.loop(0, 8)
-    def _(i):
-        rows = pl.ds(pl.multiple_of(i * 64, 64), 64)
-        w_all[dd, pl.ds(pl.multiple_of(tt * FEAT + i * 64, 64), 64), :] = quantized_rows(
-            w_slice[rows, :].astype(F32), w_peak
-        )
+    def quantize_weights(d):
+        @pl.loop(0, 4)
+        def _(i):
+            rows = pl.ds(pl.multiple_of(i * 128, 128), 128)
+            to = pl.ds(pl.multiple_of(tt * FEAT + i * 128, 128), 128)
+            w_all[d, to, :] = quantized_rows(w_raw[d, rows, :].astype(F32), w_peak)
+
+    quantize_weights(dd)
 
     def unit_a(d, t):
         return w_all.at[d, pl.ds(pl.multiple_of(t * FEAT, 16), RA)]
 
-    def unit_b(d, t):
-        return w_all.at[d, pl.ds(pl.multiple_of(t * FEAT + RA, 16), FEAT - RA)]
+    def part_a(d, t, low, high):
+        return w_all.at[d, pl.ds(pl.multiple_of(t * FEAT + low, 16), high - low)]
 
     def bundle_b(t):
         return w_all.at[:, pl.ds(pl.multiple_of(t * FEAT + RA, 16), FEAT - RA)]
@@ -337,7 +357,7 @@
     down = {0: 0, 1: 2, 2: 4, 3: 6}
     x_left, x_right, x_far, b_up, b_down, a_up, a_down = {}, {}, {}, {}, {}, {}, {}
 
-    w_send = copies.sender(w_all.at[:, pl.ds(0, 31 * FEAT // NDP)])
+    w_send = copies.sender(w_all.at[:, pl.ds(0, 28 * FEAT // NDP)])
 
     def w_go(ref, to, landing):
         return copies.start_one(ref, ref, to, w_send, landing)
@@ -360,22 +380,13 @@
     def b_send_down(step):
         b_down[step + 1] = w_go(bundle_b(zt(step)), {"tp": zt(-1)}, bundle_b(zt(step + 1)))
 
-    own_b = unit_b(dd, tt)
-    bx_left = w_go(own_b, {"dp": xd(1)}, unit_b(xd(-1), tt))
-    bx_right = w_go(own_b, {"dp": xd(-1)}, unit_b(xd(1), tt))
     a_send_up(0)
     a_send_down(0)
-    x_sends(0)
-
-    bx_far = []
-
-    def ev_bx():
-        bx_left()
-        bx_far.append(w_go(unit_b(xd(-1), tt), {"dp": xd(1)}, unit_b(xd(2), tt)))
-        bx_right()
 
     def ev_b0():
-        bx_far[0]()
+        for arrival in raw_far:
+            arrival()
+        quantize_weights(xd(2))
         b_send_up(0)
         b_send_down(0)
 
@@ -407,60 +418,35 @@
     def ev_x(j):
         def go():
             t_j = zt(rel[j])
+            cut = {7: RA // 2}.get(j, RA if j % 2 == 0 else 0)
             x_left[j]()
-            if j % 2 == 0:
-                x_far[j] = w_go(unit_a(xd(-1), t_j), {"dp": xd(1)}, unit_a(xd(2), t_j))
+            x_far[j] = []
+            if cut > 0:
+                x_far[j].append(w_go(part_a(xd(-1), t_j, 0, cut), {"dp": xd(1)}, part_a(xd(2), t_j, 0, cut)))
             x_right[j]()
-            if j % 2 == 1:
-                x_far[j] = w_go(unit_a(xd(1), t_j), {"dp": xd(-1)}, unit_a(xd(2), t_j))
+            if cut < RA:
+                x_far[j].append(w_go(part_a(xd(1), t_j, cut, RA), {"dp": xd(-1)}, part_a(xd(2), t_j, cut, RA)))
 
         return go
-
-    events = [
-        ev_bx,
-        ev_a(1),
-        ev_x(0),
-        ev_b0,
-        ev_a(2),
-        ev_x(1),
-        ev_x(2),
-        ev_b(1),
-        ev_a(3),
-        ev_x(3),
-        ev_b(2),
-        ev_a(4),
-        ev_x(4),
-        ev_x(5),
-        ev_b(3),
-        ev_x(6),
-        ev_x(7),
-        ev_b(4),
-    ]
-    done = [0]
-
-    def progress(upto):
-        while done[0] < min(upto, len(events)):
-            events[done[0]]()
-            done[0] += 1
 
     kv.x0()
     attend_if_before(sid(0, 1))
     kv.low()
+    raw_forward()
     attend_if_before(sid(-1, 0))
     kv.high()
-    progress(2)
     attend_if_before(sid(1, 0))
     kv.x3()
-    progress(4)
     attend_if_before(sid(-1, 1))
     kv.far()
-    progress(5)
+    ev_a(1)()
+    quantize_weights(xd(-1))
+    quantize_weights(xd(1))
     kv.x5()
     attend_if_before(sid(1, 1))
-    progress(6)
     attend_if_before(sid(2, 0))
     kv.x7()
-    progress(8)
+    ev_b0()
     attend_if_before(sid(2, 1))
 
     tiles[49] = jnp.zeros((8, 128), F32)
@@ -483,15 +469,19 @@
                 recv,
             )
         a_moves.append(lambda recv=recv, seven=seven: copies.arrived(recv, seven))
+        if part == 0:
+            ev_a(2)()
         z_buf[part, tt] = att_buf[pl.ds(pl.multiple_of(tt * OWN + part * HALF, HALF), HALF), :]
-    progress(10)
+    ev_x(1)()
     a_top()
     tiles[50] = max_of_tiles(16)
     tiles[24 + ss] = tiles[50]
     s_top = spread_tile(50, 24, "seq", sq)
-    progress(12)
+    ev_x(2)()
+    ev_b(1)()
     s_top()
     a_peak = jnp.max(max_of_tiles(24))
+    ev_x(3)()
 
     acts = []
     for part in range(2):
@@ -514,7 +504,8 @@
                 act_all.at[pl.ds(0, NSEQ - 1), part],
             )
         )
-        progress(13 + 2 * part)
+        if part == 0:
+            ev_a(3)()
 
     part_seven = part_buf.at[pl.ds(0, NSEQ - 1)]
     out_send, out_recv = copies.sender(part_seven), copies.receiver()
@@ -522,49 +513,48 @@
     def sub_of(i):
         return lax.rem(dd + i + lax.div(i, 2) - 2 * lax.div(i, 3), NDP)
 
-    def project(dy, first, count):
-        chip = lax.rem(yy + dy + 4, 4)
-
-        @pl.loop(first, first + count)
-        def _(i):
+    def project(first, count):
+        @pl.loop(0, 4 * count)
+        def _(n):
+            i = first + lax.div(n, 4)
+            chip = lax.rem(yy + 2 + n, 4)
             lhs = act_all[pl.ds(chip * 2, 2)].reshape(2 * OWN, NTP * FEAT)
             prod = jnp.dot(lhs, w_all[sub_of(i)], preferred_element_type=F32).astype(BF16)
             out_buf[chip * 2, i] = prod[:OWN]
             out_buf[chip * 2 + 1, i] = prod[OWN:]
 
         subs = pl.ds(first, count)
-        for dc in range(2):
-            to = sid(dy, dc)
-            if dy == 0 and dc == 0:
-                part_buf[ss, first : first + count] = out_buf[ss, first : first + count]
-            else:
-                copies.start(out_buf.at[to, subs], part_buf.at[ss, subs], {"seq": to}, out_send, out_recv)
+        for dy in (2, 1, -1, 0):
+            for dc in range(2):
+                to = sid(dy, dc)
+                if dy == 0 and dc == 0:
+                    part_buf[ss, first : first + count] = out_buf[ss, first : first + count]
+                else:
+                    copies.start(out_buf.at[to, subs], part_buf.at[ss, subs], {"seq": to}, out_send, out_recv)
 
     acts[0].low()
     acts[0].high()
-    progress(16)
+    ev_b(2)()
+    ev_a(4)()
+    ev_x(4)()
     acts[1].low()
     acts[1].high()
-    progress(17)
+    ev_x(5)()
     acts[0].far()
-    progress(len(events))
+    ev_b(3)()
+    acts[1].far()
+    ev_x(6)()
+    ev_b(4)()
     for a in acts:
-        a.x0()
-    project(0, 0, 3)
-    acts[1].far()
-    for a in acts:
-        a.x3()
-    project(-1, 0, 3)
-    for a in acts:
-        a.x5()
-    project(1, 0, 3)
-    for a in acts:
-        a.x7()
-    project(2, 0, 3)
-    for j in range(8):
-        x_far[j]()
-    for dy in (2, -1, 1, 0):
-        project(dy, 3, 1)
+        for arrival in (a.x0, a.x3, a.x5, a.x7):
+            arrival()
+    project(0, 1)
+    ev_x(7)()
+    project(1, 2)
+    for arrivals in x_far.values():
+        for arrival in arrivals:
+            arrival()
+    project(3, 1)
     loads[8].wait()
     copies.arrived(out_recv, part_seven)
 
@@ -608,7 +598,8 @@
 TILES = 8
 
 
-def quantize_kernel(hid_ref, root_ref, gain_ref, top_ref, new_ref, next_ref):
+def quantize_kernel(hid_ref, root_ref, gain_ref, top_ref, new_ref, next_ref, gain_buf):
+    gain_buf[...] = gain_ref[...].astype(F32)
     peak = jnp.max(top_ref[...])
     pick = pick_matrix()
     root = root_ref[...]
@@ -620,7 +611,7 @@
             cols.append(pl.ds(pl.multiple_of((i * TILES + n) * 128, 128), 128))
             hid = hid_ref[:, cols[n]]
             new_ref[:, cols[n]] = hid.astype(BF16)
-            gain = gain_ref[pl.ds(i * TILES + n, 1), :].astype(F32)
+            gain = gain_buf[pl.ds(i * TILES + n, 1), :]
             pieces.append(hid * root * gain)
         for n, x in enumerate(quantized_lanes(pieces, peak, pick)):
             next_ref[:, cols[n]] = x
@@ -629,7 +620,7 @@
 def local(queries, keys, values, out_weight, residual, norm_gain):
     any_space = pl.BlockSpec(memory_space=pl.ANY)
     vmem = pl.BlockSpec(memory_space=pltpu.VMEM)
-    gain = norm_gain.reshape(D // 128, 128).astype(F32)
+    gain = norm_gain.reshape(D // 128, 128)
     hid, root, top = pl.pallas_call(
         kernel,
         out_shape=(
@@ -643,7 +634,7 @@
             pltpu.VMEM((TOK, FEAT), BF16),
             pltpu.VMEM((NSEQ, 2, TOK, HEAD), BF16),
             pltpu.VMEM((FEAT, D), BF16),
-            pltpu.VMEM((FEAT, SUB), BF16),
+            pltpu.VMEM((NDP, FEAT, SUB), BF16),
             pltpu.VMEM((NDP, NTP * FEAT, SUB), BF16),
             pltpu.VMEM((HEAD, TOK), BF16),
             pltpu.VMEM((HEADS, 1, TOK), F32),
@@ -680,6 +671,7 @@
             pl.BlockSpec((8, 128), lambda i: (0, 0)),
         ],
         out_specs=(wide, wide),
+        scratch_shapes=[pltpu.VMEM((D // STEPS // 128, 128), F32)],
     )(hid, root, gain, top)
 
 

time: 112 us -> 105 us (0.938)
  Pallas kernels: 110 us -> 105 us
  other arithmetic: 1.34 us -> 0 us
    pallas_call x1, Pallas kernels: 102 us -> 97.1 us  [local(): pl.pallas_call(kernel, out_shape=(jax.ShapeDtypeStruct((OWN, D), F32), ja...]
    convert_element_type x1 -> x0, other arithmetic: 1.34 us -> none  [local(): gain = norm_gain.reshape(D // 128, 128).astype(F32)]
where the time goes in v3:
time: 105 us
  Pallas kernels  105 us (100%)
    pallas_call x1, Pallas kernels, local(): pl.pallas_call(kernel, out_shape=(jax.ShapeDtypeStruct((OWN, D), F32), ja...  97.1 us
    pallas_call x1, Pallas kernels, local(): pl.pallas_call(quantize_kernel, grid=(STEPS,), out_shape=(out, out), in_s...  7.37 us

profile of v3, /device:TPU:1, one launch (start us, length us, event | category | flops | bytes accessed | tf_op | source)
XLA Modules:
  0.0 105.1 jit_solution(13470751155944946860)
XLA Ops:
  0.6 97.1 %shard_map.77 = (f32[64,8192]{1,0:T(8,128)}, f32[64,128]{1,0:T(8,128)}, f32[8,128]{1,0:T(8,128)}) custom-call(bf16[512,512]{1,0:T(8,128)(2,1)} %q_hbm.1, bf16[512,128]{1,0:T(8,128)(2,1)} %k_hbm.1, bf16[512,128]{1,0:T(8,128)(2,1)} %v_hbm.1, bf16[512,8192]{1,0:T(8,128)(2,1)} %w_hbm.1, bf16[64,8192]{1,0:T(8,128)(2,1)} %res_hbm.1, bf16[64,128]{1,0:T(8,128)(2,1)} %bitcast.1), custom_call_target="tpu_custom_call" | custom-call | tf_op jit(solution)/shard_map/pallas_call | solution.py:624
  97.8 7.4 %shard_map.78 = (bf16[64,8192]{1,0:T(8,128)(2,1)}, bf16[64,8192]{1,0:T(8,128)(2,1)}) custom-call(f32[64,8192]{1,0:T(8,128)} %get-tuple-element.5.hid_ref, f32[64,128]{1,0:T(8,128)} %get-tuple-element.6.root_ref, bf16[64,128]{1,0:T(8,128)(2,1)} %bitcast.2, f32[8,128]{1,0:T(8,128)} %get-tuple-element.7.top_ref), custom_call_target="tpu_custom_call" | custom-call | tf_op jit(solution)/shard_map/pallas_call | solution.py:663

commit v4 on v3

--- a/solution.py
+++ b/solution.py
@@ -121,7 +121,7 @@
 
 
 N_SEND = 13
-N_RECV = 72
+N_RECV = 74
 
 
 def kernel(
@@ -349,8 +349,8 @@
     def part_a(d, t, low, high):
         return w_all.at[d, pl.ds(pl.multiple_of(t * FEAT + low, 16), high - low)]
 
-    def bundle_b(t):
-        return w_all.at[:, pl.ds(pl.multiple_of(t * FEAT + RA, 16), FEAT - RA)]
+    def part_b(t, low, high):
+        return w_all.at[:, pl.ds(pl.multiple_of(t * FEAT + low, 16), high - low)]
 
     rel = (0, -1, 1, -2, 2, -3, 3, -4)
     up = {0: 0, 1: 1, 2: 3, 3: 5, 4: 7}
@@ -369,16 +369,24 @@
         x_right[j] = w_go(own, {"dp": xd(-1)}, unit_a(xd(1), t_j))
 
     def a_send_up(step):
-        a_up[step + 1] = w_go(unit_a(dd, zt(-step)), {"tp": zt(1)}, unit_a(dd, zt(-step - 1)))
+        cut = RA // 2 if step == 3 else RA
+        landing = part_a(dd, zt(-step - 1), 0, cut)
+        a_up[step + 1] = w_go(part_a(dd, zt(-step), 0, cut), {"tp": zt(1)}, landing)
 
     def a_send_down(step):
-        a_down[step + 1] = w_go(unit_a(dd, zt(step)), {"tp": zt(-1)}, unit_a(dd, zt(step + 1)))
+        cut = RA // 2 if step == 3 else 0
+        landing = part_a(dd, zt(step + 1), cut, RA)
+        a_down[step + 1] = w_go(part_a(dd, zt(step), cut, RA), {"tp": zt(-1)}, landing)
 
     def b_send_up(step):
-        b_up[step + 1] = w_go(bundle_b(zt(-step)), {"tp": zt(1)}, bundle_b(zt(-step - 1)))
+        cut = (RA + FEAT) // 2 if step == 3 else FEAT
+        landing = part_b(zt(-step - 1), RA, cut)
+        b_up[step + 1] = w_go(part_b(zt(-step), RA, cut), {"tp": zt(1)}, landing)
 
     def b_send_down(step):
-        b_down[step + 1] = w_go(bundle_b(zt(step)), {"tp": zt(-1)}, bundle_b(zt(step + 1)))
+        cut = (RA + FEAT) // 2 if step == 3 else RA
+        landing = part_b(zt(step + 1), cut, FEAT)
+        b_down[step + 1] = w_go(part_b(zt(step), cut, FEAT), {"tp": zt(-1)}, landing)
 
     a_send_up(0)
     a_send_down(0)
@@ -391,29 +399,24 @@
         b_send_down(0)
 
     def ev_a(step):
-        def go():
-            a_up[step]()
-            if step < 4:
-                a_send_up(step)
+        a_up[step]()
+        if step < 4:
+            a_send_up(step)
             x_sends(up[step])
-            if step < 4:
-                a_down[step]()
-                if step < 3:
-                    a_send_down(step)
-                x_sends(down[step])
-
-        return go
+        a_down[step]()
+        if step < 4:
+            a_send_down(step)
+            x_sends(down[step])
+        else:
+            x_sends(up[step])
 
     def ev_b(step):
-        def go():
-            b_up[step]()
-            if step < 4:
-                b_send_up(step)
-                b_down[step]()
-                if step < 3:
-                    b_send_down(step)
-
-        return go
+        b_up[step]()
+        if step < 4:
+            b_send_up(step)
+        b_down[step]()
+        if step < 4:
+            b_send_down(step)
 
     def ev_x(j):
         def go():
@@ -432,21 +435,21 @@
     kv.x0()
     attend_if_before(sid(0, 1))
     kv.low()
+    kv.high()
     raw_forward()
     attend_if_before(sid(-1, 0))
-    kv.high()
     attend_if_before(sid(1, 0))
     kv.x3()
     attend_if_before(sid(-1, 1))
     kv.far()
-    ev_a(1)()
+    ev_a(1)
     quantize_weights(xd(-1))
     quantize_weights(xd(1))
+    ev_b0()
     kv.x5()
     attend_if_before(sid(1, 1))
     attend_if_before(sid(2, 0))
     kv.x7()
-    ev_b0()
     attend_if_before(sid(2, 1))
 
     tiles[49] = jnp.zeros((8, 128), F32)
@@ -469,16 +472,15 @@
                 recv,
             )
         a_moves.append(lambda recv=recv, seven=seven: copies.arrived(recv, seven))
-        if part == 0:
-            ev_a(2)()
         z_buf[part, tt] = att_buf[pl.ds(pl.multiple_of(tt * OWN + part * HALF, HALF), HALF), :]
+    ev_a(2)
     ev_x(1)()
     a_top()
     tiles[50] = max_of_tiles(16)
     tiles[24 + ss] = tiles[50]
     s_top = spread_tile(50, 24, "seq", sq)
     ev_x(2)()
-    ev_b(1)()
+    ev_b(1)
     s_top()
     a_peak = jnp.max(max_of_tiles(24))
     ev_x(3)()
@@ -505,7 +507,7 @@
             )
         )
         if part == 0:
-            ev_a(3)()
+            ev_x(4)()
 
     part_seven = part_buf.at[pl.ds(0, NSEQ - 1)]
     out_send, out_recv = copies.sender(part_seven), copies.receiver()
@@ -513,48 +515,50 @@
     def sub_of(i):
         return lax.rem(dd + i + lax.div(i, 2) - 2 * lax.div(i, 3), NDP)
 
-    def project(first, count):
-        @pl.loop(0, 4 * count)
+    def project(i, low, high):
+        @pl.loop(low, high)
         def _(n):
-            i = first + lax.div(n, 4)
-            chip = lax.rem(yy + 2 + n, 4)
+            chip = lax.rem(yy + 1 + 2 * n - lax.div(n, 2), 4)
             lhs = act_all[pl.ds(chip * 2, 2)].reshape(2 * OWN, NTP * FEAT)
             prod = jnp.dot(lhs, w_all[sub_of(i)], preferred_element_type=F32).astype(BF16)
             out_buf[chip * 2, i] = prod[:OWN]
             out_buf[chip * 2 + 1, i] = prod[OWN:]
 
-        subs = pl.ds(first, count)
-        for dy in (2, 1, -1, 0):
+        for dy in (1, -1, 0, 2)[low:high]:
             for dc in range(2):
                 to = sid(dy, dc)
                 if dy == 0 and dc == 0:
-                    part_buf[ss, first : first + count] = out_buf[ss, first : first + count]
+                    part_buf[ss, i] = out_buf[ss, i]
                 else:
-                    copies.start(out_buf.at[to, subs], part_buf.at[ss, subs], {"seq": to}, out_send, out_recv)
-
+                    copies.start(out_buf.at[to, i], part_buf.at[ss, i], {"seq": to}, out_send, out_recv)
+
+    ev_a(3)
     acts[0].low()
     acts[0].high()
-    ev_b(2)()
-    ev_a(4)()
-    ev_x(4)()
+    ev_b(2)
     acts[1].low()
     acts[1].high()
+    ev_a(4)
     ev_x(5)()
     acts[0].far()
-    ev_b(3)()
+    ev_b(3)
     acts[1].far()
     ev_x(6)()
-    ev_b(4)()
+    ev_b(4)
     for a in acts:
-        for arrival in (a.x0, a.x3, a.x5, a.x7):
+        for arrival in (a.x0, a.x3, a.x5):
             arrival()
-    project(0, 1)
+    project(0, 0, 3)
+    for a in acts:
+        a.x7()
+    project(0, 3, 4)
     ev_x(7)()
-    project(1, 2)
+    project(1, 0, 4)
+    project(2, 0, 4)
     for arrivals in x_far.values():
         for arrival in arrivals:
             arrival()
-    project(3, 1)
+    project(3, 0, 4)
     loads[8].wait()
     copies.arrived(out_recv, part_seven)
 

time: 105 us -> 101 us (0.962)
  Pallas kernels: 105 us -> 101 us
    pallas_call x1, Pallas kernels: 97.1 us -> 93.2 us  [local(): pl.pallas_call(kernel, out_shape=(jax.ShapeDtypeStruct((OWN, D), F32), ja...]
where the time goes in v4:
time: 101 us
  Pallas kernels  101 us (100%)
    pallas_call x1, Pallas kernels, local(): pl.pallas_call(kernel, out_shape=(jax.ShapeDtypeStruct((OWN, D), F32), ja...  93.2 us
    pallas_call x1, Pallas kernels, local(): pl.pallas_call(quantize_kernel, grid=(STEPS,), out_shape=(out, out), in_s...  7.37 us

profile of v4, /device:TPU:1, one launch (start us, length us, event | category | flops | bytes accessed | tf_op | source)
XLA Modules:
  0.0 101.2 jit_solution(5293383573320148607)
XLA Ops:
  0.6 93.2 %shard_map.77 = (f32[64,8192]{1,0:T(8,128)}, f32[64,128]{1,0:T(8,128)}, f32[8,128]{1,0:T(8,128)}) custom-call(bf16[512,512]{1,0:T(8,128)(2,1)} %q_hbm.1, bf16[512,128]{1,0:T(8,128)(2,1)} %k_hbm.1, bf16[512,128]{1,0:T(8,128)(2,1)} %v_hbm.1, bf16[512,8192]{1,0:T(8,128)(2,1)} %w_hbm.1, bf16[64,8192]{1,0:T(8,128)(2,1)} %res_hbm.1, bf16[64,128]{1,0:T(8,128)(2,1)} %bitcast.1), custom_call_target="tpu_custom_call" | custom-call | tf_op jit(solution)/shard_map/pallas_call | solution.py:628
  93.8 7.4 %shard_map.78 = (bf16[64,8192]{1,0:T(8,128)(2,1)}, bf16[64,8192]{1,0:T(8,128)(2,1)}) custom-call(f32[64,8192]{1,0:T(8,128)} %get-tuple-element.5.hid_ref, f32[64,128]{1,0:T(8,128)} %get-tuple-element.6.root_ref, bf16[64,128]{1,0:T(8,128)(2,1)} %bitcast.2, f32[8,128]{1,0:T(8,128)} %get-tuple-element.7.top_ref), custom_call_target="tpu_custom_call" | custom-call | tf_op jit(solution)/shard_map/pallas_call | solution.py:667

commit v5 on v4

--- a/solution.py
+++ b/solution.py
@@ -58,16 +58,18 @@
     return rounded(x, jnp.broadcast_to(scale * (2.0 * tensor_scale), x.shape)).reshape(n, cols)
 
 
-def quantized_lanes(pieces, peak, pick):
+def lane_tops(x):
+    top = jnp.abs(x)
+    for sh in (1, 2, 4, 8):
+        top = jnp.maximum(top, pltpu.roll(top, sh, 1))
+    return top
+
+
+def quantized_lanes(pieces, tops, peak, pick):
     rows = pieces[0].shape[0]
     tensor_scale = peak / (6.0 * 448.0)
     inverse = 1.0 / (6.0 * tensor_scale)
-    scales = []
-    for x in pieces:
-        top = jnp.abs(x)
-        for sh in (1, 2, 4, 8):
-            top = jnp.maximum(top, pltpu.roll(top, sh, 1))
-        scales.append(jnp.maximum(top * inverse, FLOOR).astype(BF16))
+    scales = [jnp.maximum(top * inverse, FLOOR).astype(BF16) for top in tops]
     spread = jnp.dot(jnp.concatenate(scales, axis=0), pick, preferred_element_type=F32)
     return [
         rounded(x, spread[i * rows : (i + 1) * rows] * (2.0 * tensor_scale)) for i, x in enumerate(pieces)
@@ -132,7 +134,8 @@
     res_hbm,
     gain_ref,
     hid_ref,
-    root_ref,
+    tops_ref,
+    new_ref,
     top_ref,
     q_buf,
     kv_buf,
@@ -152,7 +155,8 @@
     hid_buf,
     tiles,
     pick_buf,
-    root_buf,
+    tops_buf,
+    new_buf,
     send_sems,
     recv_sems,
     local_sems,
@@ -496,7 +500,8 @@
                 for g in range(GROUP)
                 for n in range(FEAT // 128)
             ]
-            for n, x in enumerate(quantized_lanes(pieces, a_peak, pick_buf[...])):
+            tops = [lane_tops(x) for x in pieces]
+            for n, x in enumerate(quantized_lanes(pieces, tops, a_peak, pick_buf[...])):
                 act_all[ss, part, :, pl.ds(pl.multiple_of(i * GROUP * FEAT + n * 128, 128), 128)] = x
 
         acts.append(
@@ -568,72 +573,80 @@
             cols = pl.ds(pl.multiple_of(i * COLS + sub_of(j) * SUB, SUB), SUB)
             hid = res_buf[:, cols].astype(F32) + part_buf[i, j].astype(F32)
             hid_buf[:, cols] = hid
+            new_buf[:, cols] = hid.astype(BF16)
             sqr = hid * hid
             for n in range(SUB // 128):
                 square = square + sqr[:, n * 128 : (n + 1) * 128]
-    store = pltpu.make_async_copy(hid_buf, hid_ref, local_sems.at[9])
-    store.start()
+    stores = [pltpu.make_async_copy(new_buf, new_ref, local_sems.at[9])]
+    stores[0].start()
     mean = jnp.sum(square, axis=1, keepdims=True) * (1.0 / D)
-    root = jnp.broadcast_to(lax.rsqrt(mean + 1e-05), (OWN, 128))
-    root_buf[...] = root
-    store_root = pltpu.make_async_copy(root_buf, root_ref, local_sems.at[10])
-    store_root.start()
+    root = lax.rsqrt(mean + 1e-05)
     top = jnp.zeros((OWN, 128), F32)
     for i in range(D // 128):
-        top = jnp.maximum(top, jnp.abs(hid_buf[:, i * 128 : (i + 1) * 128] * root * gain_ref[i : i + 1, :].astype(F32)))
+        cols = slice(i * 128, (i + 1) * 128)
+        normed = hid_buf[:, cols] * root * gain_ref[i : i + 1, :].astype(F32)
+        hid_buf[:, cols] = normed
+        top = jnp.maximum(top, jnp.abs(normed))
     tiles[51] = jnp.max(top.reshape(OWN // 8, 8, 128), axis=0)
     tiles[32 + tt] = tiles[51]
-    spread_tile(51, 32, "tp", zt)()
+    n_top = spread_tile(51, 32, "tp", zt)
+    stores.append(pltpu.make_async_copy(hid_buf, hid_ref, local_sems.at[10]))
+    stores[1].start()
+
+    @pl.loop(0, D // 128 // TILES)
+    def _(i):
+        for n in range(TILES):
+            cols = pl.ds(pl.multiple_of((i * TILES + n) * 128, 128), 128)
+            tops_buf[:, cols] = lane_tops(hid_buf[:, cols])
+
+    stores.append(pltpu.make_async_copy(tops_buf, tops_ref, local_sems.at[11]))
+    stores[2].start()
+    n_top()
     tiles[52] = max_of_tiles(32)
     tiles[40 + ss] = tiles[52]
     spread_tile(52, 40, "seq", sq)()
     tiles[53] = max_of_tiles(40)
-    store_top = pltpu.make_async_copy(tiles.at[53], top_ref, local_sems.at[11])
-    store_top.start()
+    stores.append(pltpu.make_async_copy(tiles.at[53], top_ref, local_sems.at[12]))
+    stores[3].start()
 
     assert len(copies.sent) == N_SEND and copies.n_recv == N_RECV
     copies.finish()
-    store.wait()
-    store_root.wait()
-    store_top.wait()
+    for store in stores:
+        store.wait()
 
 
 STEPS = 4
 TILES = 8
 
 
-def quantize_kernel(hid_ref, root_ref, gain_ref, top_ref, new_ref, next_ref, gain_buf):
-    gain_buf[...] = gain_ref[...].astype(F32)
+def quantize_kernel(hid_ref, tops_ref, sum_ref, top_ref, new_ref, next_ref):
     peak = jnp.max(top_ref[...])
     pick = pick_matrix()
-    root = root_ref[...]
 
     @pl.loop(0, D // STEPS // 128 // TILES)
     def _(i):
-        pieces, cols = [], []
-        for n in range(TILES):
-            cols.append(pl.ds(pl.multiple_of((i * TILES + n) * 128, 128), 128))
-            hid = hid_ref[:, cols[n]]
-            new_ref[:, cols[n]] = hid.astype(BF16)
-            gain = gain_buf[pl.ds(i * TILES + n, 1), :]
-            pieces.append(hid * root * gain)
-        for n, x in enumerate(quantized_lanes(pieces, peak, pick)):
-            next_ref[:, cols[n]] = x
+        cols = [pl.ds(pl.multiple_of((i * TILES + n) * 128, 128), 128) for n in range(TILES)]
+        pieces = [hid_ref[:, c] for c in cols]
+        tops = [tops_ref[:, c] for c in cols]
+        for c, x in zip(cols, quantized_lanes(pieces, tops, peak, pick)):
+            next_ref[:, c] = x
+            new_ref[:, c] = sum_ref[:, c]
 
 
 def local(queries, keys, values, out_weight, residual, norm_gain):
     any_space = pl.BlockSpec(memory_space=pl.ANY)
     vmem = pl.BlockSpec(memory_space=pltpu.VMEM)
     gain = norm_gain.reshape(D // 128, 128)
-    hid, root, top = pl.pallas_call(
+    hid, tops, new, top = pl.pallas_call(
         kernel,
         out_shape=(
             jax.ShapeDtypeStruct((OWN, D), F32),
-            jax.ShapeDtypeStruct((OWN, 128), F32),
+            jax.ShapeDtypeStruct((OWN, D), F32),
+            jax.ShapeDtypeStruct((OWN, D), BF16),
             jax.ShapeDtypeStruct((8, 128), F32),
         ),
         in_specs=[any_space] * 5 + [vmem],
-        out_specs=(any_space, any_space, any_space),
+        out_specs=(any_space,) * 4,
         scratch_shapes=[
             pltpu.VMEM((TOK, FEAT), BF16),
             pltpu.VMEM((NSEQ, 2, TOK, HEAD), BF16),
@@ -653,10 +666,11 @@
             pltpu.VMEM((OWN, D), F32),
             pltpu.VMEM((56, 8, 128), F32),
             pltpu.VMEM((128, 128), BF16),
-            pltpu.VMEM((OWN, 128), F32),
+            pltpu.VMEM((OWN, D), F32),
+            pltpu.VMEM((OWN, D), BF16),
             pltpu.SemaphoreType.DMA((N_SEND,)),
             pltpu.SemaphoreType.DMA((N_RECV,)),
-            pltpu.SemaphoreType.DMA((12,)),
+            pltpu.SemaphoreType.DMA((13,)),
         ],
         compiler_params=pltpu.CompilerParams(
             collective_id=0, has_side_effects=True, vmem_limit_bytes=60 * 1024 * 1024
@@ -668,15 +682,9 @@
         quantize_kernel,
         grid=(STEPS,),
         out_shape=(out, out),
-        in_specs=[
-            wide,
-            pl.BlockSpec((OWN, 128), lambda i: (0, 0)),
-            pl.BlockSpec((D // STEPS // 128, 128), lambda i: (i, 0)),
-            pl.BlockSpec((8, 128), lambda i: (0, 0)),
-        ],
+        in_specs=[wide, wide, wide, pl.BlockSpec((8, 128), lambda i: (0, 0))],
         out_specs=(wide, wide),
-        scratch_shapes=[pltpu.VMEM((D // STEPS // 128, 128), F32)],
-    )(hid, root, gain, top)
+    )(hid, tops, new, top)
 
 
 def solution(mesh):

time: 101 us -> 101 us (level)
  Pallas kernels: 101 us -> 99.7 us
where the time goes in v5:
time: 101 us; the launch traced here: 100 us
  Pallas kernels  99.7 us (99%)
    pallas_call x1, Pallas kernels, local(): pl.pallas_call(kernel, out_shape=(jax.ShapeDtypeStruct((OWN, D), F32), ja...  93.3 us
    pallas_call x1, Pallas kernels, local(): pl.pallas_call(quantize_kernel, grid=(STEPS,), out_shape=(out, out), in_s...  6.38 us

profile of v5, /device:TPU:1, one launch (start us, length us, event | category | flops | bytes accessed | tf_op | source)
XLA Modules:
  0.0 100.3 jit_solution(2335187923519186698)
XLA Ops:
  0.6 93.3 %shard_map.77 = (f32[64,8192]{1,0:T(8,128)}, f32[64,8192]{1,0:T(8,128)}, bf16[64,8192]{1,0:T(8,128)(2,1)}, f32[8,128]{1,0:T(8,128)}) custom-call(bf16[512,512]{1,0:T(8,128)(2,1)} %q_hbm.1, bf16[512,128]{1,0:T(8,128)(2,1)} %k_hbm.1, bf16[512,128]{1,0:T(8,128)(2,1)} %v_hbm.1, bf16[512,8192]{1,0:T(8,128)(2,1)} %w_hbm.1, bf16[64,8192]{1,0:T(8,128)(2,1)} %res_hbm.1, ...), custom_call_target="tpu_custom_call" | custom-call | tf_op jit(solution)/shard_map/pallas_call | solution.py:640
  93.9 6.4 %shard_map.78 = (bf16[64,8192]{1,0:T(8,128)(2,1)}, bf16[64,8192]{1,0:T(8,128)(2,1)}) custom-call(f32[64,8192]{1,0:T(8,128)} %get-tuple-element.6.hid_ref, f32[64,8192]{1,0:T(8,128)} %get-tuple-element.7.tops_ref, bf16[64,8192]{1,0:T(8,128)(2,1)} %get-tuple-element.8.sum_ref, f32[8,128]{1,0:T(8,128)} %get-tuple-element.9.top_ref), custom_call_target="tpu_custom_call" | custom-call | tf_op jit(solution)/shard_map/pallas_call | solution.py:681

commit v6 on v5

--- a/solution.py
+++ b/solution.py
@@ -563,7 +563,8 @@
     for arrivals in x_far.values():
         for arrival in arrivals:
             arrival()
-    project(3, 0, 4)
+    project(3, 3, 4)
+    project(3, 0, 3)
     loads[8].wait()
     copies.arrived(out_recv, part_seven)
 

time: 101 us -> 101 us (level)
  no operation moved by 1% of the time
where the time goes in v6:
time: 101 us; the launch traced here: 100 us
  Pallas kernels  99.8 us (99%)
    pallas_call x1, Pallas kernels, local(): pl.pallas_call(kernel, out_shape=(jax.ShapeDtypeStruct((OWN, D), F32), ja...  93.4 us
    pallas_call x1, Pallas kernels, local(): pl.pallas_call(quantize_kernel, grid=(STEPS,), out_shape=(out, out), in_s...  6.38 us

profile of v6, /device:TPU:1, one launch (start us, length us, event | category | flops | bytes accessed | tf_op | source)
XLA Modules:
  0.0 100.4 jit_solution(9882294394196877816)
XLA Ops:
  0.6 93.4 %shard_map.77 = (f32[64,8192]{1,0:T(8,128)}, f32[64,8192]{1,0:T(8,128)}, bf16[64,8192]{1,0:T(8,128)(2,1)}, f32[8,128]{1,0:T(8,128)}) custom-call(bf16[512,512]{1,0:T(8,128)(2,1)} %q_hbm.1, bf16[512,128]{1,0:T(8,128)(2,1)} %k_hbm.1, bf16[512,128]{1,0:T(8,128)(2,1)} %v_hbm.1, bf16[512,8192]{1,0:T(8,128)(2,1)} %w_hbm.1, bf16[64,8192]{1,0:T(8,128)(2,1)} %res_hbm.1, ...), custom_call_target="tpu_custom_call" | custom-call | tf_op jit(solution)/shard_map/pallas_call | solution.py:641
  94.0 6.4 %shard_map.78 = (bf16[64,8192]{1,0:T(8,128)(2,1)}, bf16[64,8192]{1,0:T(8,128)(2,1)}) custom-call(f32[64,8192]{1,0:T(8,128)} %get-tuple-element.6.hid_ref, f32[64,8192]{1,0:T(8,128)} %get-tuple-element.7.tops_ref, bf16[64,8192]{1,0:T(8,128)(2,1)} %get-tuple-element.8.sum_ref, f32[8,128]{1,0:T(8,128)} %get-tuple-element.9.top_ref), custom_call_target="tpu_custom_call" | custom-call | tf_op jit(solution)/shard_map/pallas_call | solution.py:682
